TPU v7x, 256 devices: a whole 4x4x8 slice. The times are simulated.
256 devices in a mesh: grp: 8 (over z_hi, x), slab: 32 (over z_lo, y, core).
Axes of the slice: x: 4, y: 4, z: 8 (z_hi: 2, z_lo: 4; z = z_hi * 4 + z_lo), core: 2. Of those that a mesh axis runs over, the one named last changes fastest.
Arguments:
- sample_xy: float32 [8, 32, 8, 2, 256], P('grp', 'slab'), may hold values from 0 to 384
- sample_dz: float32 [8, 32, 8, 256], P('grp', 'slab'), may hold values from 0 to 1
- sample_values: float32 [8, 32, 8, 2, 256], P('grp', 'slab'), may hold values from -6 to 6
- block_tile: int32 [8, 32, 8], P('grp', 'slab'), may hold values from 0 to 5
- block_count: int32 [8, 32, 8], P('grp', 'slab'), may hold values from 1 to 256
Outputs:
- grid_sum: float32 [384, 192, 2, 384], P('grp', 'slab')
Inputs may be any that keep to these rules, and one draw needn't show every extreme that they name: `block_tile`: the base plane of every sample of a block. Slots from block_count on hold values that are not used.
All inputs are finite; a program needn't handle non-finite values.
Results may differ from a plain program's by a relative error of at most 0.0037.
Values sent between devices are 32-bit elements; how exact they have to be, the bound alone decides.
A program may use at most 192 MiB of HBM per device.

v0:
```python
import math

import jax
import jax.numpy as jnp
from jax import lax
from jax.sharding import PartitionSpec as P

NX = 384
NY = 384
BLOCK = 256
PLANES = 6


BETA = math.pi * math.sqrt(19.45)


def from_behind(value, axis, steps):
    count = lax.axis_size(axis)
    pairs = [(source, (source + steps) % count) for source in range(count)]
    return lax.ppermute(value, axis, pairs)


def kaiser_top():
    half_sq = (0.5 * BETA) ** 2
    term = 1.0
    total = 1.0
    for order in range(1, 32):
        term = term * half_sq / (order * order)
        total = total + term
    return total - 1.0


def bessel_zero(arg):
    half_sq = 0.5 * arg * (0.5 * arg)
    term = jnp.ones_like(arg)
    total = term
    for order in range(1, 32):
        term = term * half_sq / float(order * order)
        total = total + term
    return total


def kaiser(distance):
    inside = jnp.maximum(1.0 - (distance / 3.0) ** 2, 0.0)
    bessel = bessel_zero(BETA * jnp.sqrt(inside))
    return (bessel - 1.0) / kaiser_top()


def periodic(distance, period):
    return jnp.mod(distance + 0.5 * period, period) - 0.5 * period


def spread(row_count, coords, depths, values, tile_ids, counts):
    blocks = coords.shape[0]
    block_len = coords.shape[2]
    planes = PLANES + 5
    rows_x = lax.iota(jnp.int32, row_count).astype(jnp.float32)
    cols_y = lax.iota(jnp.int32, NY).astype(jnp.float32)
    along_x = coords[:, 0].reshape(-1)
    along_y = coords[:, 1].reshape(-1)
    weight_x = kaiser(periodic(rows_x[:, None] - along_x[None, :], NX)).astype(jnp.bfloat16)
    weight_y = kaiser(periodic(cols_y[None, :] - along_y[:, None], NY)).reshape(
        blocks, block_len, 1, 1, NY
    )
    levels = (lax.iota(jnp.int32, planes) - 2).astype(jnp.float32)
    offset_z = levels[None, None, :] - (
        tile_ids.astype(jnp.float32)[:, None, None] + depths[:, :, None]
    )
    lane_ids = lax.iota(jnp.int32, block_len)
    keep_mask = (lane_ids[None, :] < counts[:, None]).astype(jnp.float32)
    weight_z = kaiser(offset_z) * keep_mask[:, :, None]
    spread_w = (
        weight_z[:, :, :, None, None] * jnp.swapaxes(values, 1, 2)[:, :, None, :, None] * weight_y
    ).astype(jnp.bfloat16)
    spread_w = spread_w.reshape(blocks * block_len, planes * 2 * NY)
    return jnp.dot(weight_x, spread_w, preferred_element_type=jnp.float32)


def add_rims(inner_planes, from_below, from_above):
    inner_planes = inner_planes.at[:, :3].add(from_below)
    return inner_planes.at[:, PLANES - 2 :].add(from_above)


def shards(sample_xy, sample_dz, sample_values, block_tile, block_count):
    planes = PLANES + 5
    own_xy = sample_xy.reshape(-1, 2, BLOCK)
    own_dz = sample_dz.reshape(-1, BLOCK)
    own_values = sample_values.reshape(-1, 2, BLOCK)
    own_tiles = block_tile.reshape(-1)
    own_counts = block_count.reshape(-1)
    full_grid = spread(NX, own_xy, own_dz, own_values, own_tiles, own_counts).reshape(
        NX, planes, 2, NY
    )
    low_rim = full_grid[:, :2]
    high_rim = full_grid[:, 2 + PLANES :]
    from_below = from_behind(high_rim, "slab", 1)
    from_above = from_behind(low_rim, "slab", -1)
    inner_planes = add_rims(full_grid[:, 2 : 2 + PLANES], from_below, from_above)
    return lax.psum_scatter(inner_planes, "grp", scatter_dimension=0, tiled=True)


def solution(mesh):
    return jax.shard_map(
        shards,
        mesh=mesh,
        in_specs=(
            P("grp", "slab", None, None, None),
            P("grp", "slab", None, None),
            P("grp", "slab", None, None, None),
            P("grp", "slab", None),
            P("grp", "slab", None),
        ),
        out_specs=P("grp", "slab", None, None),
        check_vma=False,
    )
```

profile of v0, /device:TPU:1, one launch (start us, length us, event | category | flops | bytes accessed | tf_op | source)
XLA Modules:
  0.0 323.8 jit_solution(2584350226897820477)
XLA Ops:
  6.5 0.0 reduce-scatter.2.cloned.1.call-start
  6.5 0.7 convert_bitcast_fusion
  7.2 0.7 copy.6
  7.9 0.8 fusion.108
  8.7 0.8 bitcast_add_fusion
  9.5 0.4 add_multiply_fusion.1
  10.0 13.1 %add_multiply_fusion = f32[8,256,384]{1,0,2:T(8,128)S(1)} fusion(f32[8,256]{1,0:T(8,128)S(1)} %bitcast.30, f32[384]{0:T(512)S(1)} %iota_convert_fusion), kind=kLoop, calls=%fused_computation.21 | loop fusion | flops 84934656 | bytes 3155456 | tf_op jit(solution)/shard_map/div | solution.py:46
  23.1 11.8 %multiply_convert_fusion = bf16[8,256,11,2,384]{1,0,4,3,2:T(8,128)(2,1)} fusion(f32[8,256,384]{1,0,2:T(8,128)S(1)} %add_multiply_fusion, f32[8,256,11,2]{1,0,3,2:T(8,128)S(1)} %broadcast_multiply_fusion), kind=kLoop, calls=%fused_computation | loop fusion | flops 34603008 | bytes 37928960 | tf_op jit(solution)/shard_map/convert_element_type | solution.py:74
  34.8 23.7 %copy.10 = bf16[1056,8,8,256]{3,1,2,0:T(8,128)(2,1)} copy(bf16[1056,8,8,256]{3,2,1,0:T(8,128)(2,1)} %bitcast.28) | data formatting | bytes 69206016
  58.5 38.8 %fusion.25 = f32[384,11,2,384]{3,0,2,1:T(8,128)S(1)} fusion(bf16[11,2,384,2048]{3,2,1,0:T(8,128)(2,1)} %bitcast.29, f32[2048]{0:T(1024)S(1)} %bitcast.33, f32[384]{0:T(512)S(1)} %iota_convert_fusion), kind=kOutput, calls=%fused_computation.34 | convolution fusion | flops 13373276160 | bytes 47588864 | tf_op jit(solution)/shard_map/dot_general | solution.py:76
  97.3 0.2 slice.85
  97.6 2.7 collective-permute-start
  100.2 0.2 slice.87
  100.4 0.6 collective-permute-start.1
  101.0 3.4 %slice.83 = f32[384,6,2,384]{3,0,2,1:T(8,128)} slice(f32[384,11,2,384]{3,0,2,1:T(8,128)S(1)} %fusion.25), slice={[0:384], [2:8], [0:2], [0:384]} | slice | bytes 14155776 | tf_op jit(solution)/shard_map/slice | solution.py:98
  104.4 34.2 %collective-permute-done = f32[384,3,2,384]{3,0,2,1:T(8,128)S(1)} collective-permute-done((f32[384,3,2,384]{3,0,2,1:T(8,128)S(1)}, f32[384,3,2,384]{3,0,2,1:T(8,128)S(1)}, u32[]{:S(2)}, u32[]{:S(2)}) %collective-permute-start) | collective-permute-done | bytes 3538976 | tf_op jit(solution)/shard_map/ppermute | solution.py:20
  138.7 2.1 fusion
  140.8 0.0 collective-permute-done.1
  140.8 3.4 %fusion.23 = f32[384,6,2,384]{3,0,2,1:T(8,128)} fusion(f32[384,6,2,384]{3,0,2,1:T(8,128)} %fusion, f32[384,2,2,384]{3,0,2,1:T(8,128)S(1)} %collective-permute-done.1), kind=kLoop, calls=%fused_computation.32 | loop fusion | flops 589824 | bytes 7077888 | tf_op jit(solution)/shard_map/scatter-add | solution.py:81
  144.2 0.0 reduce-scatter.2.cloned.1.call-update
  144.2 170.2 %reduce-scatter.2.cloned.1.call-done = f32[48,6,2,384]{3,0,2,1:T(8,128)} async-done(((f32[384,6,2,384]{3,0,2,1:T(8,128)}), f32[48,6,2,384]{3,0,2,1:T(8,128)}) %reduce-scatter.2.cloned.1.call-update) | async-done | bytes 884752 | tf_op jit(solution)/shard_map/reduce_scatter | solution.py:99
  314.4 2.5 copy.7
  (4 shorter events, 0.0 us)
Async XLA Ops:
  6.5 307.9 %reduce-scatter.2.cloned.1.call-start = ((), (), s32[]{:S(2)}) async-start(), calls=%async_computation.1 | async-start | bytes 7962624 | tf_op jit(solution)/shard_map/reduce_scatter | solution.py:99
  97.6 41.1 %collective-permute-start = (f32[384,3,2,384]{3,0,2,1:T(8,128)S(1)}, f32[384,3,2,384]{3,0,2,1:T(8,128)S(1)}, u32[]{:S(2)}, u32[]{:S(2)}) collective-permute-start(f32[384,3,2,384]{3,0,2,1:T(8,128)S(1)} %slice.85), channel_id=1, source_target_pairs={{0,1},{1,2},{2,3},{3,4},{4,5},{5,6},{6,7},{7,8},{8,9},{9,10},{10,1... | collective-permute-start | bytes 10616840 | tf_op jit(solution)/shard_map/ppermute | solution.py:20
  100.4 40.4 %collective-permute-start.1 = (f32[384,2,2,384]{3,0,2,1:T(8,128)S(1)}, f32[384,2,2,384]{3,0,2,1:T(8,128)S(1)}, u32[]{:S(2)}, u32[]{:S(2)}) collective-permute-start(f32[384,2,2,384]{3,0,2,1:T(8,128)S(1)} %slice.87), channel_id=1, source_target_pairs={{0,31},{1,0},{2,1},{3,2},{4,3},{5,4},{6,5},{7,6},{8,7},{9,8},{10,9... | collective-permute-start | bytes 7077896 | tf_op jit(solution)/shard_map/ppermute | solution.py:20
Sparse Core Ops, SparseCore 0:
  144.4 170.0 reduce-scatter.1
where the time goes:
time: 325 us; the launch traced here: 324 us
  waiting for transfers between devices  204 us (63%)
  matrix products  38.8 us (12%)
  other arithmetic  32.3 us (10%)
  local copies, waits for them, and re-layouts  31.5 us (10%)
  between operations  13.4 us (4%)
  starting transfers between devices  3.3 us (1%)
    reduce_scatter x1, waiting for transfers between devices, shards(): lax.psum_scatter(inner_planes, 'grp', scatter_dimension=0, tiled=True)  170 us
    dot_general x1, matrix products, spread(): return jnp.dot(weight_x, spread_w, preferred_element_type=jnp.float32)  38.8 us
    ppermute x2, waiting for transfers between devices, from_behind(): return lax.ppermute(value, axis, pairs)  34.2 us
    unnamed x2, local copies, waits for them, and re-layouts  23.7 us
    div x1, other arithmetic, kaiser(): return (bessel - 1.0) / kaiser_top()  13.1 us
    convert_element_type x1, other arithmetic, spread(): spread_w = (weight_z[:, :, :, None, None] * jnp.swapaxes(values, 1, 2)[:,...  11.8 us
  transfers between devices with their start and end apart: 3, of which 2 were waited for; matrix products, arithmetic and copies ran while one was open for 2% of the time, Pallas kernels for 0%

commit v1 on v0

v1 whole, which is shorter than its diff:
```python
import math

import jax
import jax.numpy as jnp
from jax import lax
from jax.experimental import pallas as pl
from jax.experimental.pallas import tpu as pltpu
from jax.sharding import PartitionSpec as P

NX = 384
NY = 384
PLANES = 6
BLOCKS = 8
GROUPS = 8
ROWS = 48
FIELDS = 6
HALF_ROWS = FIELDS * BLOCKS
SEND_ROWS = 2 * HALF_ROWS
MESH = pl.DeviceIdType.MESH
BETA = math.pi * math.sqrt(19.45)
F32 = jnp.float32
BF16 = jnp.bfloat16
I32 = jnp.int32


def kaiser_coefficients():
    half_sq = (0.5 * BETA) ** 2
    terms = []
    term = 1.0
    for order in range(1, 32):
        term = term * half_sq / (order * order)
        terms.append(term)
    top = sum(terms)
    return [value / top for value in terms]


COEFF = kaiser_coefficients()


def kaiser(distance):
    third = distance * (1.0 / 3.0)
    inside = jnp.maximum(1.0 - third * third, 0.0)
    square = inside * inside
    fourth = square * square
    chains = []
    for first in range(4):
        picked = COEFF[first::4]
        total = jnp.full_like(inside, picked[-1])
        for value in picked[-2::-1]:
            total = total * fourth + value
        chains.append(total)
    low = chains[0] + chains[1] * inside
    high = chains[2] + chains[3] * inside
    return (low + high * square) * inside


def sort_kernel(tile_ref, count_ref, xy_ref, dz_ref, val_ref, out_ref, fields):
    lanes = lax.broadcasted_iota(I32, (BLOCKS, 256), 1)
    subs = lax.broadcasted_iota(I32, (BLOCKS, 256), 0)
    counts = jnp.zeros((BLOCKS, 256), I32)
    tiles = jnp.zeros((BLOCKS, 256), I32)
    for b in range(BLOCKS):
        counts = jnp.where(subs == b, count_ref[0, 0, b], counts)
        tiles = jnp.where(subs == b, tile_ref[0, 0, b], tiles)
    along_x = xy_ref[:, 0, :]
    cell = jnp.floor(along_x)
    shifted = cell + 3.0
    shifted = jnp.where(shifted >= NX, shifted - NX, shifted)
    shifted = jnp.where(lanes < counts, shifted, 400.0)
    fields[0:8] = along_x
    fields[8:16] = xy_ref[:, 1, :]
    fields[16:24] = dz_ref[...]
    fields[24:32] = val_ref[:, 0, :]
    fields[32:40] = val_ref[:, 1, :]
    table = jnp.where(lanes == 17, tiles.astype(F32), 0.0)
    for at in range(17):
        if at < 8:
            bound = float(ROWS * at)
        elif at < 16:
            bound = float(ROWS * (at - 8) + ROWS + 5)
        else:
            bound = 5.0
        below = jnp.sum(jnp.where(shifted < bound, 1.0, 0.0), axis=1, keepdims=True)
        table = jnp.where(lanes == at, below, table)
    key = shifted * 256.0 + lanes.astype(F32)
    key_t = key.T
    place = lax.broadcasted_iota(I32, (256, 256), 0).astype(F32)
    for b in range(BLOCKS):
        before = key_t[:, b : b + 1] < key[b : b + 1, :]
        rank = jnp.sum(jnp.where(before, 1.0, 0.0), axis=0, keepdims=True)
        pick = jnp.where(place == rank, 1.0, 0.0).astype(BF16)
        rows = jnp.concatenate([fields[f * 8 + b : f * 8 + b + 1, :] for f in range(5)] + [jnp.zeros((3, 256), F32)], axis=0)
        top = rows.astype(BF16)
        rest = rows - top.astype(F32)
        mid = rest.astype(BF16)
        low = (rest - mid.astype(F32)).astype(BF16)
        parts = jnp.concatenate([top.astype(F32), mid.astype(F32), low.astype(F32)], axis=0).astype(BF16)
        moved = lax.dot_general(parts, pick, (((1,), (1,)), ((), ())), preferred_element_type=F32)
        ordered = (moved[0:8] + moved[8:16]) + moved[16:24]
        for f in range(5):
            for half in range(2):
                out_ref[half * HALF_ROWS + f * 8 + b : half * HALF_ROWS + f * 8 + b + 1, :] = ordered[
                    f : f + 1, half * 128 : half * 128 + 128
                ]
    out_ref[40:48, :] = table[:, 0:128]
    out_ref[HALF_ROWS + 40 : HALF_ROWS + 48, :] = table[:, 128:256]


def sort_blocks(tile, count, xy, dz, val):
    smem = pl.BlockSpec(memory_space=pltpu.SMEM)
    vmem = pl.BlockSpec(memory_space=pltpu.VMEM)
    return pl.pallas_call(
        sort_kernel,
        out_shape=jax.ShapeDtypeStruct((SEND_ROWS, 128), F32),
        in_specs=[smem, smem, vmem, vmem, vmem],
        out_specs=vmem,
        scratch_shapes=[pltpu.VMEM((40, 256), F32)],
        name="sort_blocks",
    )(tile, count, xy, dz, val)


def exchange_kernel(own_ref, out_ref, send_sem, recv_sem, copy_sem):
    grp = lax.axis_index("grp")
    slab = lax.axis_index("slab")
    far = lax.rem(grp + 4, 8)
    half = (grp // 4) * 4
    spot = grp - half
    peers = [half + lax.rem(spot + step, 4) for step in (1, 3, 2)]
    far_half = 4 - half
    up = lax.rem(slab + 1, 32)
    down = lax.rem(slab + 31, 32)
    around = [(far, slab)] + [(peer, slab) for peer in peers] + [(grp, up), (grp, down)]

    barrier = pltpu.get_barrier_semaphore()
    for device in around:
        pl.semaphore_signal(barrier, inc=1, device_id=device, device_id_type=MESH)

    own_copy = pltpu.make_async_copy(own_ref, out_ref.at[0, grp], copy_sem)
    own_copy.start()
    pl.semaphore_wait(barrier, len(around))

    sends = []

    def send(source, kind, owner, sem, device):
        copy = pltpu.make_async_remote_copy(
            src_ref=source,
            dst_ref=out_ref.at[kind, owner],
            send_sem=send_sem.at[len(sends)],
            recv_sem=recv_sem.at[sem],
            device_id=device,
            device_id_type=MESH,
        )
        copy.start()
        sends.append(copy)
        return copy

    def arrive(kind, owner, sem):
        pltpu.make_async_remote_copy(
            src_ref=own_ref,
            dst_ref=out_ref.at[kind, owner],
            send_sem=send_sem.at[0],
            recv_sem=recv_sem.at[sem],
            device_id=(grp, slab),
            device_id_type=MESH,
        ).wait_recv()

    send(own_ref, 0, grp, 0, (far, slab))
    for at, peer in enumerate(peers):
        send(own_ref, 0, grp, 1 + at, (peer, slab))
    send(own_ref, 1, grp, 7, (grp, up))
    send(own_ref, 2, grp, 15, (grp, down))
    back = [half + lax.rem(spot + step, 4) for step in (3, 1, 2)]
    for at in range(3):
        arrive(0, back[at], 1 + at)
        send(out_ref.at[0, back[at]], 1, back[at], 8 + at, (grp, up))
        send(out_ref.at[0, back[at]], 2, back[at], 16 + at, (grp, down))
    arrive(0, far, 0)
    for at, peer in enumerate(peers):
        send(out_ref.at[0, far], 0, far, 4 + at, (peer, slab))
    send(out_ref.at[0, far], 1, far, 11, (grp, up))
    send(out_ref.at[0, far], 2, far, 19, (grp, down))
    for at in range(3):
        owner = back[at] - half + far_half
        arrive(0, owner, 4 + at)
        send(out_ref.at[0, owner], 1, owner, 12 + at, (grp, up))
        send(out_ref.at[0, owner], 2, owner, 20 + at, (grp, down))
    for kind, base in ((1, 7), (2, 15)):
        arrive(kind, grp, base)
        arrive(kind, far, base + 4)
        for at in range(3):
            arrive(kind, back[at], base + 1 + at)
            arrive(kind, back[at] - half + far_half, base + 5 + at)
    own_copy.wait()
    for copy in sends:
        copy.wait_send()


def exchange(own):
    vmem = pl.BlockSpec(memory_space=pltpu.VMEM)
    return pl.pallas_call(
        exchange_kernel,
        out_shape=jax.ShapeDtypeStruct((3, GROUPS, SEND_ROWS, 128), F32),
        in_specs=[pl.BlockSpec(memory_space=pl.ANY)],
        out_specs=vmem,
        scratch_shapes=[pltpu.SemaphoreType.DMA((23,)), pltpu.SemaphoreType.DMA((23,)), pltpu.SemaphoreType.DMA],
        compiler_params=pltpu.CompilerParams(collective_id=0, has_side_effects=True),
        name="exchange",
    )(own)


def grid_kernel(read_group, all_ref, out_ref, table_v, table, packed, lhs, rhs, total, sem):
    group = read_group()
    sources = 3 * GROUPS
    for source in range(sources):
        table_v[source * 8 : source * 8 + 8, :] = all_ref[source * SEND_ROWS + 40 : source * SEND_ROWS + 48, :].astype(I32)
    copy = pltpu.make_async_copy(table_v, table, sem)
    copy.start()
    total[...] = jnp.zeros_like(total)
    lanes = lax.broadcasted_iota(I32, (8, 128), 1)
    subs = lax.broadcasted_iota(I32, (8, 128), 0)
    copy.wait()

    def depth_shift(kind, tile):
        return tile + (0, -PLANES, PLANES)[kind]

    def wanted(kind, tile):
        return (True, tile >= 3, tile <= 1)[kind]

    def append(kind, source, b, half, low, count, offset):
        tile = table[source * 8 + b, 17]
        values = all_ref[pl.ds(source * SEND_ROWS + half * HALF_ROWS + b, FIELDS, stride=8), :]
        values = jnp.where(subs[:FIELDS] == 2, values + depth_shift(kind, tile).astype(F32), values)
        at = lax.bitwise_and(offset, 127)
        rolled = pltpu.roll(values, lax.bitwise_and(at - low + 128, 127), 1)
        slot = lax.shift_right_logical(offset, 7)
        packed[slot, 0:FIELDS] = jnp.where(lanes[:FIELDS] >= at, rolled, packed[slot, 0:FIELDS])
        packed[slot + 1, 0:FIELDS] = rolled
        return offset + count

    def window(kind, source, b):
        row = source * 8 + b
        start = table[row, group]
        count = table[row, 8 + group] - start
        if kind > 0:
            count = jnp.where(wanted(kind, table[row, 17]), count, 0)
        half = jnp.minimum(lax.shift_right_logical(start, 7), 1)
        low = lax.bitwise_and(start, 127)
        first = jnp.minimum(count, 128 - low)
        return half, low, first, count - first

    def gather_first(kind):
        def body(at, carry):
            offset, more = carry
            source = kind * GROUPS + at
            for b in range(BLOCKS):
                half, low, first, left = window(kind, source, b)
                offset = append(kind, source, b, half, low, first, offset)
                more = more + left
            return offset, more

        return body

    offset = jnp.int32(0)
    for kind in range(3):
        offset, more = lax.fori_loop(0, GROUPS, gather_first(kind), (offset, jnp.int32(0)))

        def gather_rest(at, offset):
            source = kind * GROUPS + lax.shift_right_logical(at, 3)
            b = lax.bitwise_and(at, 7)
            left = window(kind, source, b)[3]
            return lax.cond(left > 0, lambda o: append(kind, source, b, 1, 0, left, o), lambda o: o, offset)

        offset = lax.fori_loop(0, jnp.where(more > 0, 64, 0), gather_rest, offset)

        def gather_wrap(at, offset):
            source = kind * GROUPS + lax.shift_right_logical(at, 3)
            b = lax.bitwise_and(at, 7)
            row = source * 8 + b
            count = table[row, 16]
            if kind > 0:
                count = jnp.where(wanted(kind, table[row, 17]), count, 0)

            def add(o):
                o = append(kind, source, b, 0, 0, jnp.minimum(count, 128), o)
                left = count - jnp.minimum(count, 128)
                return lax.cond(left > 0, lambda p: append(kind, source, b, 1, 0, left, p), lambda p: p, o)

            return lax.cond(count > 0, add, lambda o: o, offset)

        offset = lax.fori_loop(0, jnp.where(group == GROUPS - 1, 64, 0), gather_wrap, offset)

    subs_f = subs.astype(F32)
    first_row = (group * ROWS).astype(F32)

    def pick(weights, index):
        return jnp.take_along_axis(weights, index, axis=0, mode="promise_in_bounds")

    def chunk(at, carry):
        for half in range(2):
            cols = slice(half * 128, half * 128 + 128)
            values = packed[at * 2 + half]
            values = jnp.where(lanes + (at * 256 + half * 128) < offset, values, 0.0)
            along_x, along_y, along_z = [jnp.broadcast_to(values[f : f + 1], (8, 128)) for f in range(3)]
            cell_x = jnp.floor(along_x)
            cell_y = jnp.floor(along_y)
            taps_x = kaiser(subs_f - 2.0 - (along_x - cell_x))
            taps_y = kaiser(subs_f - 2.0 - (along_y - cell_y))
            taps_z = kaiser(subs_f - along_z)
            base_x = cell_x - 2.0 - first_row
            base_x = jnp.where(base_x < -192.0, base_x + NX, base_x)
            base_x = jnp.where(base_x >= 192.0, base_x - NX, base_x)
            base_y = cell_y - 2.0
            base_y = jnp.where(base_y < 0.0, base_y + NY, base_y)
            base_y = jnp.where(base_y >= NY, base_y - NY, base_y)
            away_x = subs - base_x.astype(I32)
            away_y = subs - base_y.astype(I32)

            def spread(taps, away, rows, wrap):
                index = away + rows
                if wrap:
                    index = jnp.where(index < 0, index + NY, index)
                else:
                    index = jnp.where(index < 0, 7, index)
                return pick(taps, jnp.minimum(index, 7))

            for row in range(0, NY, 16):
                pair = [spread(taps_y, away_y, row + part, row + part == 0) for part in (0, 8)]
                rhs[row : row + 16, cols] = jnp.concatenate(pair, axis=0).astype(BF16)
            weights_x = [spread(taps_x, away_x, row, False).astype(BF16).astype(F32) for row in range(0, ROWS, 8)]
            for z in range(PLANES):
                for c in range(2):
                    scale = jnp.broadcast_to(taps_z[z : z + 1] * values[3 + c : 4 + c], (8, 128))
                    for row in range(0, ROWS, 16):
                        pair = [weights_x[(row + part) // 8] * scale for part in (0, 8)]
                        first = (z * 2 + c) * ROWS + row
                        lhs[first : first + 16, cols] = jnp.concatenate(pair, axis=0).astype(BF16)
        total[...] += lax.dot_general(lhs[...], rhs[...], (((1,), (1,)), ((), ())), preferred_element_type=F32)
        return carry

    lax.fori_loop(0, lax.shift_right_logical(offset + 255, 8), chunk, 0)
    for z in range(PLANES):
        for c in range(2):
            for y in range(3):
                first = (z * 2 + c) * ROWS
                out_ref[pl.ds(z * 6 + y * 2 + c, ROWS, stride=36), :] = total[first : first + ROWS, y * 128 : y * 128 + 128]


def grid_block(everything, group=None):
    vmem = pl.BlockSpec(memory_space=pltpu.VMEM)
    if group is None:
        operands, specs = [everything], [vmem]

        def kernel(all_ref, *refs):
            grid_kernel(lambda: lax.axis_index("grp"), all_ref, *refs)
    else:
        operands, specs = [group, everything], [pl.BlockSpec(memory_space=pltpu.SMEM), vmem]

        def kernel(group_ref, all_ref, *refs):
            grid_kernel(lambda: group_ref[0], all_ref, *refs)

    return pl.pallas_call(
        kernel,
        out_shape=jax.ShapeDtypeStruct((ROWS * PLANES * 6, 128), F32),
        in_specs=specs,
        out_specs=vmem,
        scratch_shapes=[
            pltpu.VMEM((192, 128), I32),
            pltpu.SMEM((192, 128), I32),
            pltpu.VMEM((388, 8, 128), F32),
            pltpu.VMEM((12 * ROWS, 256), BF16),
            pltpu.VMEM((NY, 256), BF16),
            pltpu.VMEM((12 * ROWS, NY), F32),
            pltpu.SemaphoreType.DMA,
        ],
        name="grid_block",
    )(*operands)


def finish(flat):
    return flat.reshape(ROWS, PLANES, 3, 2, 128).transpose(0, 1, 3, 2, 4).reshape(ROWS, PLANES, 2, NY)


def shards(sample_xy, sample_dz, sample_values, block_tile, block_count):
    own = sort_blocks(
        block_tile, block_count, sample_xy.reshape(8, 2, 256), sample_dz.reshape(8, 256), sample_values.reshape(8, 2, 256)
    )
    everything = exchange(own)
    return finish(grid_block(everything.reshape(3 * GROUPS * SEND_ROWS, 128)))


def solution(mesh):
    return jax.shard_map(
        shards,
        mesh=mesh,
        in_specs=(
            P("grp", "slab", None, None, None),
            P("grp", "slab", None, None),
            P("grp", "slab", None, None, None),
            P("grp", "slab", None),
            P("grp", "slab", None),
        ),
        out_specs=P("grp", "slab", None, None),
        check_vma=False,
    )
```

time: 325 us -> 49.6 us (0.15)
  the two profiles are of different devices: /device:TPU:1 before, /device:TPU:167 now
where the time goes in v1:
time: 49.6 us; the launch traced here: 48.7 us
  Pallas kernels  45.4 us (92%)
  local copies, waits for them, and re-layouts  3.32 us (7%)
    pallas_call x1, Pallas kernels, grid_block(): pl.pallas_call(kernel, out_shape=jax.ShapeDtypeStruct((ROWS * PLANES * 6,...  25.6 us
    pallas_call x1, Pallas kernels, exchange(): pl.pallas_call(exchange_kernel, out_shape=jax.ShapeDtypeStruct((3, GROUPS...  17.6 us
    reshape x3, local copies, waits for them, and re-layouts, finish(): flat.reshape(ROWS, PLANES, 3, 2, 128).transpose(0, 1, 3, 2, 4)  3.32 us
    pallas_call x1, Pallas kernels, sort_blocks(): pl.pallas_call(sort_kernel, out_shape=jax.ShapeDtypeStruct((SEND_ROWS, 12...  2.17 us

profile of v1, /device:TPU:167, one launch (start us, length us, event | category | flops | bytes accessed | tf_op | source)
XLA Modules:
  0.0 48.7 jit_solution(3987927507655250681)
XLA Ops:
  0.0 2.2 %sort_blocks.1.own_ref = f32[96,128]{1,0:T(8,128)} custom-call(s32[1,1,8]{2,1,0:T(1,128)} %tile_ref.1, s32[1,1,8]{2,1,0:T(1,128)} %count_ref.1, f32[8,2,256]{2,1,0:T(2,128)} %bitcast.13, f32[8,256]{1,0:T(8,128)} %bitcast.15, f32[8,2,256]{2,1,0:T(2,128)} %bitcast.14), custom_call_target="tpu_custom_call" | custom-call | tf_op jit(solution)/shard_map/sort_blocks/pallas_call | solution.py:112
  2.2 17.6 %exchange.1 = f32[3,8,96,128]{3,2,1,0:T(8,128)} custom-call(f32[96,128]{1,0:T(8,128)} %sort_blocks.1.own_ref), custom_call_target="tpu_custom_call" | custom-call | tf_op jit(solution)/shard_map/exchange/pallas_call | solution.py:200
  19.8 25.6 %grid_block.1 = f32[1728,128]{1,0:T(8,128)} custom-call(f32[2304,128]{1,0:T(8,128)} %bitcast.10), custom_call_target="tpu_custom_call" | custom-call | tf_op jit(solution)/shard_map/grid_block/pallas_call | solution.py:361
  45.4 1.5 %copy.10 = f32[48,6,3,2,128]{4,2,0,3,1:T(4,128)S(1)} copy(f32[48,6,3,2,128]{4,3,2,1,0:T(2,128)} %bitcast.12) | data formatting | bytes 1769472 | tf_op jit(solution)/shard_map/reshape | solution.py:380
  46.9 0.5 reshape.23
  47.4 1.4 %copy.8 = f32[48,6,2,384]{3,2,1,0:T(2,128)} copy(f32[48,6,2,384]{3,0,2,1:T(8,128)S(1)} %reshape.23) | data formatting | bytes 1769472 | tf_op jit(solution)/shard_map/reshape | solution.py:380

commit v2 on v1

v2 whole, which is shorter than its diff:
```python
import math

import jax
import jax.numpy as jnp
from jax import lax
from jax.experimental import pallas as pl
from jax.experimental.pallas import tpu as pltpu
from jax.sharding import PartitionSpec as P

NX = 384
NY = 384
PLANES = 6
BLOCKS = 8
GROUPS = 8
ROWS = 48
FIELDS = 5
HALF_ROWS = FIELDS * BLOCKS
TABLE = 2 * HALF_ROWS
SEND_ROWS = TABLE + BLOCKS
SOURCES = 3 * GROUPS
START, COUNT, WRAP = 0, 8, 32
MESH = pl.DeviceIdType.MESH
BETA = math.pi * math.sqrt(19.45)
F32 = jnp.float32
BF16 = jnp.bfloat16
I32 = jnp.int32


def kaiser_coefficients():
    half_sq = (0.5 * BETA) ** 2
    terms = []
    term = 1.0
    for order in range(1, 32):
        term = term * half_sq / (order * order)
        terms.append(term)
    top = sum(terms)
    return [value / top for value in terms]


COEFF = kaiser_coefficients()


def kaiser(distance):
    third = distance * (1.0 / 3.0)
    inside = jnp.maximum(1.0 - third * third, 0.0)
    square = inside * inside
    fourth = square * square
    chains = []
    for first in range(4):
        picked = COEFF[first::4]
        total = jnp.full_like(inside, picked[-1])
        for value in picked[-2::-1]:
            total = total * fourth + value
        chains.append(total)
    low = chains[0] + chains[1] * inside
    high = chains[2] + chains[3] * inside
    return (low + high * square) * inside


def sort_blocks(tile_ref, count_ref, xy_ref, dz_ref, val_ref, out_ref, fields):
    lanes = lax.broadcasted_iota(I32, (BLOCKS, 256), 1)
    subs = lax.broadcasted_iota(I32, (BLOCKS, 256), 0)
    counts = jnp.zeros((BLOCKS, 256), I32)
    tiles = jnp.zeros((BLOCKS, 256), I32)
    for b in range(BLOCKS):
        counts = jnp.where(subs == b, count_ref[0, 0, b], counts)
        tiles = jnp.where(subs == b, tile_ref[0, 0, b], tiles)
    along_x = xy_ref[:, 0, :]
    cell = jnp.floor(along_x)
    shifted = cell + 3.0
    shifted = jnp.where(shifted >= NX, shifted - NX, shifted)
    shifted = jnp.where(lanes < counts, shifted, 400.0)
    fields[0:8] = along_x
    fields[8:16] = xy_ref[:, 1, :]
    fields[16:24] = dz_ref[...] + tiles.astype(F32)
    fields[24:32] = val_ref[:, 0, :]
    fields[32:40] = val_ref[:, 1, :]

    def below(bound):
        return jnp.sum(jnp.where(shifted < bound, 1.0, 0.0), axis=1, keepdims=True)

    column = lanes[:, 0:128]
    tile_f = tiles[:, 0:128].astype(F32)
    upper = jnp.where(tile_f > 2.5, 1.0, 0.0)
    lower = jnp.where(tile_f < 1.5, 1.0, 0.0)
    table = jnp.zeros((BLOCKS, 128), F32)
    for group in range(GROUPS):
        start = below(float(ROWS * group))
        count = below(float(ROWS * group + ROWS + 5)) - start
        table = jnp.where(column == START + group, start, table)
        table = jnp.where(column == COUNT + group, count, table)
        table = jnp.where(column == COUNT + 8 + group, count * upper, table)
        table = jnp.where(column == COUNT + 16 + group, count * lower, table)
    count = below(5.0)
    table = jnp.where(column == WRAP, count, table)
    table = jnp.where(column == WRAP + 1, count * upper, table)
    table = jnp.where(column == WRAP + 2, count * lower, table)
    out_ref[TABLE : TABLE + BLOCKS, :] = table
    key = shifted * 256.0 + lanes.astype(F32)
    key_t = key.T
    place = lax.broadcasted_iota(I32, (256, 256), 0).astype(F32)
    for b in range(BLOCKS):
        before = key_t[:, b : b + 1] < key[b : b + 1, :]
        rank = jnp.sum(jnp.where(before, 1.0, 0.0), axis=0, keepdims=True)
        pick = jnp.where(place == rank, 1.0, 0.0).astype(BF16)
        rows = jnp.concatenate([fields[f * 8 + b : f * 8 + b + 1, :] for f in range(5)] + [jnp.zeros((3, 256), F32)], axis=0)
        top = rows.astype(BF16)
        rest = rows - top.astype(F32)
        mid = rest.astype(BF16)
        low = (rest - mid.astype(F32)).astype(BF16)
        parts = jnp.concatenate([top.astype(F32), mid.astype(F32), low.astype(F32)], axis=0).astype(BF16)
        moved = lax.dot_general(parts, pick, (((1,), (1,)), ((), ())), preferred_element_type=F32)
        ordered = (moved[0:8] + moved[8:16]) + moved[16:24]
        for f in range(FIELDS):
            for half in range(2):
                row = half * HALF_ROWS + f * 8 + b
                out_ref[row : row + 1, :] = ordered[f : f + 1, half * 128 : half * 128 + 128]


def exchange_kernel(tile_ref, count_ref, xy_ref, dz_ref, val_ref, out_ref, fields, own_ref, send_sem, recv_sem):
    grp = lax.axis_index("grp")
    slab = lax.axis_index("slab")
    far = lax.rem(grp + 4, 8)
    half = (grp // 4) * 4
    spot = grp - half
    peers = [half + lax.rem(spot + step, 4) for step in (1, 3, 2)]
    far_half = 4 - half
    up = lax.rem(slab + 1, 32)
    down = lax.rem(slab + 31, 32)
    around = [(far, slab)] + [(peer, slab) for peer in peers] + [(grp, up), (grp, down)]

    barrier = pltpu.get_barrier_semaphore()
    for device in around:
        pl.semaphore_signal(barrier, inc=1, device_id=device, device_id_type=MESH)
    sort_blocks(tile_ref, count_ref, xy_ref, dz_ref, val_ref, own_ref, fields)
    pl.semaphore_wait(barrier, len(around))

    sends = []

    def send(source, kind, owner, sem, device):
        copy = pltpu.make_async_remote_copy(
            src_ref=source,
            dst_ref=out_ref.at[kind, owner],
            send_sem=send_sem.at[len(sends)],
            recv_sem=recv_sem.at[sem],
            device_id=device,
            device_id_type=MESH,
        )
        copy.start()
        sends.append(copy)
        return copy

    def arrive(kind, owner, sem):
        pltpu.make_async_remote_copy(
            src_ref=own_ref,
            dst_ref=out_ref.at[kind, owner],
            send_sem=send_sem.at[0],
            recv_sem=recv_sem.at[sem],
            device_id=(grp, slab),
            device_id_type=MESH,
        ).wait_recv()

    send(own_ref, 0, grp, 0, (far, slab))
    for at, peer in enumerate(peers):
        send(own_ref, 0, grp, 1 + at, (peer, slab))
    send(own_ref, 1, grp, 7, (grp, up))
    send(own_ref, 2, grp, 15, (grp, down))
    out_ref[0, grp] = own_ref[...]
    back = [half + lax.rem(spot + step, 4) for step in (3, 1, 2)]
    for at in range(3):
        arrive(0, back[at], 1 + at)
        send(out_ref.at[0, back[at]], 1, back[at], 8 + at, (grp, up))
        send(out_ref.at[0, back[at]], 2, back[at], 16 + at, (grp, down))
    arrive(0, far, 0)
    for at, peer in enumerate(peers):
        send(out_ref.at[0, far], 0, far, 4 + at, (peer, slab))
    send(out_ref.at[0, far], 1, far, 11, (grp, up))
    send(out_ref.at[0, far], 2, far, 19, (grp, down))
    for at in range(3):
        owner = back[at] - half + far_half
        arrive(0, owner, 4 + at)
        send(out_ref.at[0, owner], 1, owner, 12 + at, (grp, up))
        send(out_ref.at[0, owner], 2, owner, 20 + at, (grp, down))
    for kind, base in ((1, 7), (2, 15)):
        arrive(kind, grp, base)
        arrive(kind, far, base + 4)
        for at in range(3):
            arrive(kind, back[at], base + 1 + at)
            arrive(kind, back[at] - half + far_half, base + 5 + at)
    for copy in sends:
        copy.wait_send()


def exchange(tile, count, xy, dz, val):
    vmem = pl.BlockSpec(memory_space=pltpu.VMEM)
    smem = pl.BlockSpec(memory_space=pltpu.SMEM)
    return pl.pallas_call(
        exchange_kernel,
        out_shape=jax.ShapeDtypeStruct((3, GROUPS, SEND_ROWS, 128), F32),
        in_specs=[smem, smem, vmem, vmem, vmem],
        out_specs=vmem,
        scratch_shapes=[
            pltpu.VMEM((HALF_ROWS, 256), F32),
            pltpu.VMEM((SEND_ROWS, 128), F32),
            pltpu.SemaphoreType.DMA((23,)),
            pltpu.SemaphoreType.DMA((23,)),
        ],
        compiler_params=pltpu.CompilerParams(collective_id=0, has_side_effects=True, vmem_limit_bytes=8 * 2**20),
        name="exchange",
    )(tile, count, xy, dz, val)


def grid_kernel(read_group, all_ref, out_ref, table_v, table, packed, lhs0, rhs0, lhs1, rhs1, total, flat, sem, out_sem):
    group = read_group()
    for source in range(SOURCES):
        first = source * SEND_ROWS + TABLE
        table_v[source * 8 : source * 8 + 8, :] = all_ref[first : first + 8, :].astype(I32)
    copy = pltpu.make_async_copy(table_v, table, sem)
    copy.start()
    total[...] = jnp.zeros_like(total)
    lhs1[...] = jnp.zeros_like(lhs1)
    rhs1[...] = jnp.zeros_like(rhs1)
    lanes = lax.broadcasted_iota(I32, (8, 128), 1)
    lanes_f = lanes[:FIELDS]
    subs = lax.broadcasted_iota(I32, (8, 128), 0)
    copy.wait()

    def append(kind, source, b, start, count, offset):
        first = source * SEND_ROWS + b
        low = lax.bitwise_and(start, 127)
        half = jnp.minimum(lax.shift_right_logical(start, 7), 1)
        values = all_ref[pl.ds(first + half * HALF_ROWS, FIELDS, stride=8), :]
        after = all_ref[pl.ds(first + HALF_ROWS, FIELDS, stride=8), :]
        values = jnp.where(lanes_f >= low, values, after)
        if kind > 0:
            values = values + jnp.where(subs[:FIELDS] == 2, (0.0, -6.0, 6.0)[kind], 0.0)
        at = lax.bitwise_and(offset, 127)
        rolled = pltpu.roll(values, lax.bitwise_and(at - low + 128, 127), 1)
        slot = lax.shift_right_logical(offset, 7)
        pltpu.store(packed.at[slot, 0:FIELDS], rolled, mask=lanes_f >= at)
        packed[slot + 1, 0:FIELDS] = rolled
        return offset + count

    def spans(kind, wrap, source, b):
        row = source * 8 + b
        if wrap:
            return 0, table[row, WRAP + kind]
        return table[row, group], table[row, COUNT + 8 * kind + group]

    def gather(kind, wrap, offset):
        def body(at, carry):
            offset, more = carry
            source = kind * GROUPS + at
            for b in range(BLOCKS):
                start, count = spans(kind, wrap, source, b)
                first = jnp.minimum(count, 128)
                offset = append(kind, source, b, start, first, offset)
                more = more + (count - first)
            return offset, more

        return body

    def gather_rest(kind, wrap):
        def body(at, offset):
            source = kind * GROUPS + lax.shift_right_logical(at, 3)
            b = lax.bitwise_and(at, 7)
            start, count = spans(kind, wrap, source, b)
            left = jnp.maximum(count - 128, 0)
            return lax.cond(left > 0, lambda o: append(kind, source, b, start + 128, left, o), lambda o: o, offset)

        return body

    offset = jnp.int32(0)
    for wrap in (False, True):
        for kind in range(3):
            steps = jnp.where(group == GROUPS - 1, GROUPS, 0) if wrap else GROUPS
            offset, more = lax.fori_loop(0, steps, gather(kind, wrap, offset), (offset, jnp.int32(0)))
            offset = lax.fori_loop(0, jnp.where(more > 0, 64, 0), gather_rest(kind, wrap), offset)

    subs_f = subs.astype(F32)
    first_row = (group * ROWS).astype(F32)

    def place(taps, base):
        away = subs_f - base
        part = -jnp.floor(away * 0.125)
        index = (away + 8.0 * part).astype(I32)
        turned = jnp.take_along_axis(taps, index, axis=0, mode="promise_in_bounds")
        part = jnp.where(part < 0.0, part + 48.0, part)
        part = jnp.where(part >= 48.0, part - 48.0, part)
        return turned, jnp.concatenate([part, part - 1.0], axis=0).astype(BF16)

    def twice(value):
        return jnp.concatenate([value, value], axis=0).astype(BF16)

    def build(lhs, rhs, at):
        for half in range(2):
            cols = slice(half * 128, half * 128 + 128)
            values = packed[at * 2 + half]
            values = jnp.where(lanes + (at * 256 + half * 128) < offset, values, 0.0)
            along_x, along_y, along_z = [jnp.broadcast_to(values[f : f + 1], (8, 128)) for f in range(3)]
            cell_x = jnp.floor(along_x)
            cell_y = jnp.floor(along_y)
            taps_x = kaiser(subs_f - 2.0 - (along_x - cell_x)).astype(BF16).astype(F32)
            taps_y = kaiser(subs_f - 2.0 - (along_y - cell_y))
            taps_z = kaiser(subs_f - along_z)
            turned_x, part_x = place(taps_x, cell_x - 2.0 - first_row)
            turned_y, part_y = place(taps_y, cell_y - 2.0)
            turned_y = twice(turned_y)
            zero = jnp.zeros((16, 128), BF16)
            for row in range(0, NY, 16):
                rhs[row : row + 16, cols] = jnp.where(part_y == row // 8, turned_y, zero)
            here = [part_x == row // 8 for row in range(0, ROWS, 16)]
            for z in range(PLANES):
                for c in range(2):
                    scale = jnp.broadcast_to(taps_z[z : z + 1] * values[3 + c : 4 + c], (8, 128))
                    scaled = twice(turned_x * scale)
                    for at_row, mask in enumerate(here):
                        first = (z * 2 + c) * ROWS + at_row * 16
                        lhs[first : first + 16, cols] = jnp.where(mask, scaled, zero)

    def multiply(lhs, rhs):
        total[...] += lax.dot_general(lhs[...], rhs[...], (((1,), (1,)), ((), ())), preferred_element_type=F32)

    def two_chunks(at, carry):
        build(lhs0, rhs0, at * 2)
        multiply(lhs1, rhs1)
        build(lhs1, rhs1, at * 2 + 1)
        multiply(lhs0, rhs0)
        return carry

    lax.fori_loop(0, lax.shift_right_logical(offset + 511, 9), two_chunks, 0)
    multiply(lhs1, rhs1)
    lines = flat.reshape(ROWS * PLANES * 6, 128)
    for z in range(PLANES):
        for c in range(2):
            for y in range(3):
                first = (z * 2 + c) * ROWS
                lines[pl.ds(z * 6 + y * 2 + c, ROWS, stride=36), :] = total[first : first + ROWS, y * 128 : y * 128 + 128]
    copies = [pltpu.make_async_copy(flat.at[:, y], out_ref.at[:, :, pl.ds(y * 128, 128)], out_sem.at[y]) for y in range(3)]
    for copy in copies:
        copy.start()
    for copy in copies:
        copy.wait()


def grid_block(everything, group=None):
    vmem = pl.BlockSpec(memory_space=pltpu.VMEM)
    if group is None:
        operands, specs = [everything], [vmem]

        def kernel(all_ref, *refs):
            grid_kernel(lambda: lax.axis_index("grp"), all_ref, *refs)
    else:
        operands, specs = [group, everything], [pl.BlockSpec(memory_space=pltpu.SMEM), vmem]

        def kernel(group_ref, all_ref, *refs):
            grid_kernel(lambda: group_ref[0], all_ref, *refs)

    return pl.pallas_call(
        kernel,
        out_shape=jax.ShapeDtypeStruct((ROWS * PLANES, 2, NY), F32),
        in_specs=specs,
        out_specs=pl.BlockSpec(memory_space=pl.ANY),
        scratch_shapes=[
            pltpu.VMEM((SOURCES * 8, 128), I32),
            pltpu.SMEM((SOURCES * 8, 128), I32),
            pltpu.VMEM((388, 8, 128), F32),
            pltpu.VMEM((12 * ROWS, 256), BF16),
            pltpu.VMEM((NY, 256), BF16),
            pltpu.VMEM((12 * ROWS, 256), BF16),
            pltpu.VMEM((NY, 256), BF16),
            pltpu.VMEM((12 * ROWS, NY), F32),
            pltpu.VMEM((ROWS * PLANES, 3, 2, 128), F32),
            pltpu.SemaphoreType.DMA,
            pltpu.SemaphoreType.DMA((3,)),
        ],
        compiler_params=pltpu.CompilerParams(vmem_limit_bytes=16 * 2**20),
        name="grid_block",
    )(*operands)


def shards(sample_xy, sample_dz, sample_values, block_tile, block_count):
    everything = exchange(
        block_tile, block_count, sample_xy.reshape(8, 2, 256), sample_dz.reshape(8, 256), sample_values.reshape(8, 2, 256)
    )
    block = grid_block(everything.reshape(SOURCES * SEND_ROWS, 128))
    return block.reshape(ROWS, PLANES, 2, NY)


def solution(mesh):
    return jax.shard_map(
        shards,
        mesh=mesh,
        in_specs=(
            P("grp", "slab", None, None, None),
            P("grp", "slab", None, None),
            P("grp", "slab", None, None, None),
            P("grp", "slab", None),
            P("grp", "slab", None),
        ),
        out_specs=P("grp", "slab", None, None),
        check_vma=False,
    )
```

time: 49.6 us -> 38.7 us (0.78)
  the two profiles are of different devices: /device:TPU:167 before, /device:TPU:1 now
where the time goes in v2:
time: 38.7 us; the launch traced here: 38.3 us
  Pallas kernels  34.9 us (90%)
  local copies, waits for them, and re-layouts  3.44 us (9%)
    pallas_call x1, Pallas kernels, exchange(): pl.pallas_call(exchange_kernel, out_shape=jax.ShapeDtypeStruct((3, GROUPS...  22.7 us
    pallas_call x1, Pallas kernels, grid_block(): pl.pallas_call(kernel, out_shape=jax.ShapeDtypeStruct((ROWS * PLANES, 2,...  12.2 us
    unnamed x10, local copies, waits for them, and re-layouts  3.44 us

profile of v2, /device:TPU:1, one launch (start us, length us, event | category | flops | bytes accessed | tf_op | source)
XLA Modules:
  0.0 38.3 jit_solution(10876692276948081085)
XLA Ops:
  0.0 0.0 copy-start
  0.0 0.7 %copy-done = f32[1,1,8,2,256]{4,3,2,1,0:T(2,128)S(1)} copy-done((f32[1,1,8,2,256]{4,3,2,1,0:T(2,128)S(1)}, f32[1,1,8,2,256]{4,3,2,1,0:T(2,128)}, u32[]{:S(2)}) %copy-start) | copy-done | bytes 16408
  0.7 0.0 copy-start.1
  0.7 0.7 %copy-done.1 = f32[1,1,8,2,256]{4,3,2,1,0:T(2,128)S(1)} copy-done((f32[1,1,8,2,256]{4,3,2,1,0:T(2,128)S(1)}, f32[1,1,8,2,256]{4,3,2,1,0:T(2,128)}, u32[]{:S(2)}) %copy-start.1) | copy-done | bytes 16408
  1.4 0.0 copy-start.2
  1.4 0.7 %copy-done.2 = f32[1,1,8,256]{3,2,1,0:T(8,128)S(1)} copy-done((f32[1,1,8,256]{3,2,1,0:T(8,128)S(1)}, f32[1,1,8,256]{3,2,1,0:T(8,128)}, u32[]{:S(2)}) %copy-start.2) | copy-done | bytes 8216
  2.1 0.0 copy-start.3
  2.1 0.7 %copy-done.3 = s32[1,1,8]{2,1,0:T(1,128)S(1)} copy-done((s32[1,1,8]{2,1,0:T(1,128)S(1)}, s32[1,1,8]{2,1,0:T(1,128)}, u32[]{:S(2)}) %copy-start.3) | copy-done | bytes 56
  2.8 0.0 copy-start.4
  2.8 0.7 %copy-done.4 = s32[1,1,8]{2,1,0:T(1,128)S(1)} copy-done((s32[1,1,8]{2,1,0:T(1,128)S(1)}, s32[1,1,8]{2,1,0:T(1,128)}, u32[]{:S(2)}) %copy-start.4) | copy-done | bytes 56
  3.4 22.7 %exchange.1 = f32[3,8,88,128]{3,2,1,0:T(8,128)S(1)} custom-call(s32[1,1,8]{2,1,0:T(1,128)S(1)} %copy-done.3, s32[1,1,8]{2,1,0:T(1,128)S(1)} %copy-done.4, f32[8,2,256]{2,1,0:T(2,128)S(1)} %bitcast.6, f32[8,256]{1,0:T(8,128)S(1)} %bitcast.8, f32[8,2,256]{2,1,0:T(2,128)S(1)} %bitcast.7), custom_call_target="tpu_custom_call" | custom-call | tf_op jit(solution)/shard_map/exchange/pallas_call | solution.py:197
  26.1 12.2 %grid_block.1 = f32[288,2,384]{2,1,0:T(2,128)} custom-call(f32[2112,128]{1,0:T(8,128)S(1)} %bitcast.5), custom_call_target="tpu_custom_call" | custom-call | tf_op jit(solution)/shard_map/grid_block/pallas_call | solution.py:359
Async XLA Ops:
  0.0 0.7 %copy-start = (f32[1,1,8,2,256]{4,3,2,1,0:T(2,128)S(1)}, f32[1,1,8,2,256]{4,3,2,1,0:T(2,128)}, u32[]{:S(2)}) copy-start(f32[1,1,8,2,256]{4,3,2,1,0:T(2,128)} %param.5) | copy-start | bytes 49156
  0.7 0.7 %copy-start.1 = (f32[1,1,8,2,256]{4,3,2,1,0:T(2,128)S(1)}, f32[1,1,8,2,256]{4,3,2,1,0:T(2,128)}, u32[]{:S(2)}) copy-start(f32[1,1,8,2,256]{4,3,2,1,0:T(2,128)} %param.7) | copy-start | bytes 49156
  1.4 0.7 %copy-start.2 = (f32[1,1,8,256]{3,2,1,0:T(8,128)S(1)}, f32[1,1,8,256]{3,2,1,0:T(8,128)}, u32[]{:S(2)}) copy-start(f32[1,1,8,256]{3,2,1,0:T(8,128)} %param.6) | copy-start | bytes 24580
  2.1 0.7 %copy-start.3 = (s32[1,1,8]{2,1,0:T(1,128)S(1)}, s32[1,1,8]{2,1,0:T(1,128)}, u32[]{:S(2)}) copy-start(s32[1,1,8]{2,1,0:T(1,128)} %tile_ref.1) | copy-start | bytes 100
  2.8 0.7 %copy-start.4 = (s32[1,1,8]{2,1,0:T(1,128)S(1)}, s32[1,1,8]{2,1,0:T(1,128)}, u32[]{:S(2)}) copy-start(s32[1,1,8]{2,1,0:T(1,128)} %count_ref.1) | copy-start | bytes 100

commit v3 on v2

--- a/solution.py
+++ b/solution.py
@@ -18,7 +18,7 @@
 TABLE = 2 * HALF_ROWS
 SEND_ROWS = TABLE + BLOCKS
 SOURCES = 3 * GROUPS
-START, COUNT, WRAP = 0, 8, 32
+START, COUNT, LEFT, WRAP, WRAP_LEFT, ANY_LEFT = 0, 8, 32, 56, 80, 104
 MESH = pl.DeviceIdType.MESH
 BETA = math.pi * math.sqrt(19.45)
 F32 = jnp.float32
@@ -81,21 +81,27 @@
 
     column = lanes[:, 0:128]
     tile_f = tiles[:, 0:128].astype(F32)
-    upper = jnp.where(tile_f > 2.5, 1.0, 0.0)
-    lower = jnp.where(tile_f < 1.5, 1.0, 0.0)
+    kinds = [jnp.ones((BLOCKS, 128), F32), jnp.where(tile_f > 2.5, 1.0, 0.0), jnp.where(tile_f < 1.5, 1.0, 0.0)]
     table = jnp.zeros((BLOCKS, 128), F32)
     for group in range(GROUPS):
         start = below(float(ROWS * group))
         count = below(float(ROWS * group + ROWS + 5)) - start
-        table = jnp.where(column == START + group, start, table)
-        table = jnp.where(column == COUNT + group, count, table)
-        table = jnp.where(column == COUNT + 8 + group, count * upper, table)
-        table = jnp.where(column == COUNT + 16 + group, count * lower, table)
+        first = jnp.minimum(count, 128.0)
+        table = jnp.where(column == START + group, jnp.minimum(start, 255.0), table)
+        for kind in range(3):
+            table = jnp.where(column == COUNT + 8 * kind + group, first * kinds[kind], table)
+            table = jnp.where(column == LEFT + 8 * kind + group, (count - first) * kinds[kind], table)
     count = below(5.0)
-    table = jnp.where(column == WRAP, count, table)
-    table = jnp.where(column == WRAP + 1, count * upper, table)
-    table = jnp.where(column == WRAP + 2, count * lower, table)
-    out_ref[TABLE : TABLE + BLOCKS, :] = table
+    first = jnp.minimum(count, 128.0)
+    for kind in range(3):
+        table = jnp.where(column == WRAP + kind, first * kinds[kind], table)
+        table = jnp.where(column == WRAP + 3 + kind, (count - first) * kinds[kind], table)
+    table = table.T
+    pieces = [table[at : at + 8] for at in range(0, WRAP, 8)]
+    pieces += [jnp.broadcast_to(table[WRAP + at : WRAP + at + 1], (8, 8)) for at in range(6)]
+    left = pieces[4] + pieces[10]
+    pieces.append(jnp.broadcast_to(jnp.sum(left, axis=1, keepdims=True), (8, 8)))
+    out_ref[TABLE : TABLE + BLOCKS, :] = jnp.concatenate(pieces + [jnp.zeros((8, 128 - 8 * len(pieces)), F32)], axis=1)
     key = shifted * 256.0 + lanes.astype(F32)
     key_t = key.T
     place = lax.broadcasted_iota(I32, (256, 256), 0).astype(F32)
@@ -117,13 +123,23 @@
                 out_ref[row : row + 1, :] = ordered[f : f + 1, half * 128 : half * 128 + 128]
 
 
-def exchange_kernel(tile_ref, count_ref, xy_ref, dz_ref, val_ref, out_ref, fields, own_ref, send_sem, recv_sem):
+def exchange_kernel(
+    tile_in, count_in, xy_in, dz_in, val_in, out_ref, tile_ref, count_ref, xy_ref, dz_ref, val_ref, fields, own_ref, in_sem, send_sem, recv_sem
+):
+    loads = [
+        pltpu.make_async_copy(source, target, in_sem.at[at])
+        for at, (source, target) in enumerate(
+            [(xy_in, xy_ref), (tile_in, tile_ref), (count_in, count_ref), (dz_in, dz_ref), (val_in, val_ref)]
+        )
+    ]
+    for load in loads:
+        load.start()
     grp = lax.axis_index("grp")
     slab = lax.axis_index("slab")
     far = lax.rem(grp + 4, 8)
     half = (grp // 4) * 4
     spot = grp - half
-    peers = [half + lax.rem(spot + step, 4) for step in (1, 3, 2)]
+    peers = [half + lax.rem(spot + step, 4) for step in (2, 1, 3)]
     far_half = 4 - half
     up = lax.rem(slab + 1, 32)
     down = lax.rem(slab + 31, 32)
@@ -132,6 +148,8 @@
     barrier = pltpu.get_barrier_semaphore()
     for device in around:
         pl.semaphore_signal(barrier, inc=1, device_id=device, device_id_type=MESH)
+    for load in loads:
+        load.wait()
     sort_blocks(tile_ref, count_ref, xy_ref, dz_ref, val_ref, own_ref, fields)
     pl.semaphore_wait(barrier, len(around))
 
@@ -166,7 +184,7 @@
     send(own_ref, 1, grp, 7, (grp, up))
     send(own_ref, 2, grp, 15, (grp, down))
     out_ref[0, grp] = own_ref[...]
-    back = [half + lax.rem(spot + step, 4) for step in (3, 1, 2)]
+    back = [half + lax.rem(spot + step, 4) for step in (2, 3, 1)]
     for at in range(3):
         arrive(0, back[at], 1 + at)
         send(out_ref.at[0, back[at]], 1, back[at], 8 + at, (grp, up))
@@ -193,15 +211,21 @@
 
 def exchange(tile, count, xy, dz, val):
     vmem = pl.BlockSpec(memory_space=pltpu.VMEM)
-    smem = pl.BlockSpec(memory_space=pltpu.SMEM)
+    hbm = pl.BlockSpec(memory_space=pltpu.HBM)
     return pl.pallas_call(
         exchange_kernel,
         out_shape=jax.ShapeDtypeStruct((3, GROUPS, SEND_ROWS, 128), F32),
-        in_specs=[smem, smem, vmem, vmem, vmem],
+        in_specs=[hbm] * 5,
         out_specs=vmem,
         scratch_shapes=[
+            pltpu.SMEM((1, 1, 8), I32),
+            pltpu.SMEM((1, 1, 8), I32),
+            pltpu.VMEM((BLOCKS, 2, 256), F32),
+            pltpu.VMEM((BLOCKS, 256), F32),
+            pltpu.VMEM((BLOCKS, 2, 256), F32),
             pltpu.VMEM((HALF_ROWS, 256), F32),
             pltpu.VMEM((SEND_ROWS, 128), F32),
+            pltpu.SemaphoreType.DMA((5,)),
             pltpu.SemaphoreType.DMA((23,)),
             pltpu.SemaphoreType.DMA((23,)),
         ],
@@ -210,16 +234,12 @@
     )(tile, count, xy, dz, val)
 
 
-def grid_kernel(read_group, all_ref, out_ref, table_v, table, packed, lhs0, rhs0, lhs1, rhs1, total, flat, sem, out_sem):
+def grid_kernel(read_group, all_ref, out_ref, table_v, table, packed, held0, held1, flat, sem, out_sem):
     group = read_group()
     for source in range(SOURCES):
-        first = source * SEND_ROWS + TABLE
-        table_v[source * 8 : source * 8 + 8, :] = all_ref[first : first + 8, :].astype(I32)
+        table_v[source : source + 1, :] = all_ref[pl.ds(source * SEND_ROWS + TABLE + group, 1), :].astype(I32)
     copy = pltpu.make_async_copy(table_v, table, sem)
     copy.start()
-    total[...] = jnp.zeros_like(total)
-    lhs1[...] = jnp.zeros_like(lhs1)
-    rhs1[...] = jnp.zeros_like(rhs1)
     lanes = lax.broadcasted_iota(I32, (8, 128), 1)
     lanes_f = lanes[:FIELDS]
     subs = lax.broadcasted_iota(I32, (8, 128), 0)
@@ -228,35 +248,27 @@
     def append(kind, source, b, start, count, offset):
         first = source * SEND_ROWS + b
         low = lax.bitwise_and(start, 127)
-        half = jnp.minimum(lax.shift_right_logical(start, 7), 1)
+        half = lax.shift_right_logical(start, 7)
         values = all_ref[pl.ds(first + half * HALF_ROWS, FIELDS, stride=8), :]
         after = all_ref[pl.ds(first + HALF_ROWS, FIELDS, stride=8), :]
         values = jnp.where(lanes_f >= low, values, after)
         if kind > 0:
             values = values + jnp.where(subs[:FIELDS] == 2, (0.0, -6.0, 6.0)[kind], 0.0)
         at = lax.bitwise_and(offset, 127)
-        rolled = pltpu.roll(values, lax.bitwise_and(at - low + 128, 127), 1)
+        rolled = pltpu.roll(values, lax.bitwise_and(at - low, 127), 1)
         slot = lax.shift_right_logical(offset, 7)
         pltpu.store(packed.at[slot, 0:FIELDS], rolled, mask=lanes_f >= at)
         packed[slot + 1, 0:FIELDS] = rolled
         return offset + count
 
-    def spans(kind, wrap, source, b):
-        row = source * 8 + b
-        if wrap:
-            return 0, table[row, WRAP + kind]
-        return table[row, group], table[row, COUNT + 8 * kind + group]
-
-    def gather(kind, wrap, offset):
+    def gather(kind, wrap):
         def body(at, carry):
             offset, more = carry
             source = kind * GROUPS + at
             for b in range(BLOCKS):
-                start, count = spans(kind, wrap, source, b)
-                first = jnp.minimum(count, 128)
-                offset = append(kind, source, b, start, first, offset)
-                more = more + (count - first)
-            return offset, more
+                start = jnp.int32(0) if wrap else table[source, START + b]
+                offset = append(kind, source, b, start, table[source, (WRAP if wrap else COUNT) + 8 * kind + b], offset)
+            return offset, more + table[source, ANY_LEFT]
 
         return body
 
@@ -264,8 +276,8 @@
         def body(at, offset):
             source = kind * GROUPS + lax.shift_right_logical(at, 3)
             b = lax.bitwise_and(at, 7)
-            start, count = spans(kind, wrap, source, b)
-            left = jnp.maximum(count - 128, 0)
+            start = jnp.int32(0) if wrap else table[source, START + b]
+            left = table[source, (WRAP_LEFT if wrap else LEFT) + 8 * kind + b]
             return lax.cond(left > 0, lambda o: append(kind, source, b, start + 128, left, o), lambda o: o, offset)
 
         return body
@@ -274,7 +286,7 @@
     for wrap in (False, True):
         for kind in range(3):
             steps = jnp.where(group == GROUPS - 1, GROUPS, 0) if wrap else GROUPS
-            offset, more = lax.fori_loop(0, steps, gather(kind, wrap, offset), (offset, jnp.int32(0)))
+            offset, more = lax.fori_loop(0, steps, gather(kind, wrap), (offset, jnp.int32(0)))
             offset = lax.fori_loop(0, jnp.where(more > 0, 64, 0), gather_rest(kind, wrap), offset)
 
     subs_f = subs.astype(F32)
@@ -287,14 +299,19 @@
         turned = jnp.take_along_axis(taps, index, axis=0, mode="promise_in_bounds")
         part = jnp.where(part < 0.0, part + 48.0, part)
         part = jnp.where(part >= 48.0, part - 48.0, part)
-        return turned, jnp.concatenate([part, part - 1.0], axis=0).astype(BF16)
+        return turned, part
+
+    def pair(part):
+        return jnp.concatenate([part, part - 1.0], axis=0).astype(BF16)
 
     def twice(value):
         return jnp.concatenate([value, value], axis=0).astype(BF16)
 
-    def build(lhs, rhs, at):
+    zero = jnp.zeros((16, 128), BF16)
+
+    def prepare(held, at):
+        sides = []
         for half in range(2):
-            cols = slice(half * 128, half * 128 + 128)
             values = packed[at * 2 + half]
             values = jnp.where(lanes + (at * 256 + half * 128) < offset, values, 0.0)
             along_x, along_y, along_z = [jnp.broadcast_to(values[f : f + 1], (8, 128)) for f in range(3)]
@@ -305,37 +322,53 @@
             taps_z = kaiser(subs_f - along_z)
             turned_x, part_x = place(taps_x, cell_x - 2.0 - first_row)
             turned_y, part_y = place(taps_y, cell_y - 2.0)
-            turned_y = twice(turned_y)
-            zero = jnp.zeros((16, 128), BF16)
-            for row in range(0, NY, 16):
-                rhs[row : row + 16, cols] = jnp.where(part_y == row // 8, turned_y, zero)
-            here = [part_x == row // 8 for row in range(0, ROWS, 16)]
-            for z in range(PLANES):
-                for c in range(2):
-                    scale = jnp.broadcast_to(taps_z[z : z + 1] * values[3 + c : 4 + c], (8, 128))
-                    scaled = twice(turned_x * scale)
-                    for at_row, mask in enumerate(here):
-                        first = (z * 2 + c) * ROWS + at_row * 16
-                        lhs[first : first + 16, cols] = jnp.where(mask, scaled, zero)
-
-    def multiply(lhs, rhs):
-        total[...] += lax.dot_general(lhs[...], rhs[...], (((1,), (1,)), ((), ())), preferred_element_type=F32)
-
-    def two_chunks(at, carry):
-        build(lhs0, rhs0, at * 2)
-        multiply(lhs1, rhs1)
-        build(lhs1, rhs1, at * 2 + 1)
-        multiply(lhs0, rhs0)
-        return carry
-
-    lax.fori_loop(0, lax.shift_right_logical(offset + 511, 9), two_chunks, 0)
-    multiply(lhs1, rhs1)
-    lines = flat.reshape(ROWS * PLANES * 6, 128)
-    for z in range(PLANES):
-        for c in range(2):
+            held[half, 0] = turned_x
+            held[half, 1] = part_x
+            for c in range(2):
+                held[half, 2 + c] = taps_z * jnp.broadcast_to(values[3 + c : 4 + c], (8, 128))
+            turned_y, part_y = twice(turned_y), pair(part_y)
+            sides.append([jnp.where(part_y == group_y, turned_y, zero) for group_y in range(0, NY // 8, 2)] + [zero] * 8)
+        for unit in range(2):
+            tiles = [jnp.concatenate([side[unit * 16 + at] for side in sides], axis=1) for at in range(16)]
+            pltpu.matmul_push_rhs(jnp.concatenate(tiles, axis=0), staging_register=0, mxu_index=unit, transpose=True)
+
+    def stream(held, sums):
+        here = []
+        for half in range(2):
+            part_x = pair(held[half, 1])
+            here.append([part_x == group_x for group_x in range(0, ROWS // 8, 2)])
+        for plane in range(2 * PLANES):
+            z, c = plane // 2, plane % 2
+            sides = []
+            for half in range(2):
+                scaled = twice(held[half, 0] * jnp.broadcast_to(held[half, 2 + c, z : z + 1], (8, 128)))
+                sides.append([jnp.where(mask, scaled, zero) for mask in here[half]])
+            rows = jnp.concatenate([jnp.concatenate([side[at] for side in sides], axis=1) for at in range(3)], axis=0)
+            for unit in range(2):
+                pltpu.matmul_acc_lhs(sums[unit][plane], rows, load_staged_rhs=0 if plane == 0 else None)
+
+    def run(*accumulators):
+        sums = (accumulators[:12], accumulators[12:])
+        prepare(held0, 0)
+
+        def two_chunks(at, carry):
+            stream(held0, sums)
+            prepare(held1, at * 2 + 1)
+            stream(held1, sums)
+            prepare(held0, at * 2 + 2)
+            return carry
+
+        lax.fori_loop(0, lax.shift_right_logical(offset + 511, 9), two_chunks, 0)
+        for unit in range(2):
+            pltpu.matmul_acc_lhs(sums[unit][0], jnp.zeros((ROWS, 256), BF16), load_staged_rhs=0)
+        lines = flat.reshape(ROWS * PLANES * 6, 128)
+        for plane in range(2 * PLANES):
+            z, c = plane // 2, plane % 2
+            sides = [pltpu.matmul_pop(sums[unit][plane]) for unit in range(2)]
             for y in range(3):
-                first = (z * 2 + c) * ROWS
-                lines[pl.ds(z * 6 + y * 2 + c, ROWS, stride=36), :] = total[first : first + ROWS, y * 128 : y * 128 + 128]
+                lines[pl.ds(z * 6 + y * 2 + c, ROWS, stride=36), :] = sides[y // 2][:, (y % 2) * 128 : (y % 2) * 128 + 128]
+
+    pl.run_scoped(run, *[pltpu.ACC(unit)((ROWS, 256), F32) for unit in range(2) for _ in range(12)])
     copies = [pltpu.make_async_copy(flat.at[:, y], out_ref.at[:, :, pl.ds(y * 128, 128)], out_sem.at[y]) for y in range(3)]
     for copy in copies:
         copy.start()
@@ -362,14 +395,11 @@
         in_specs=specs,
         out_specs=pl.BlockSpec(memory_space=pl.ANY),
         scratch_shapes=[
-            pltpu.VMEM((SOURCES * 8, 128), I32),
-            pltpu.SMEM((SOURCES * 8, 128), I32),
+            pltpu.VMEM((SOURCES, 128), I32),
+            pltpu.SMEM((SOURCES, 128), I32),
             pltpu.VMEM((388, 8, 128), F32),
-            pltpu.VMEM((12 * ROWS, 256), BF16),
-            pltpu.VMEM((NY, 256), BF16),
-            pltpu.VMEM((12 * ROWS, 256), BF16),
-            pltpu.VMEM((NY, 256), BF16),
-            pltpu.VMEM((12 * ROWS, NY), F32),
+            pltpu.VMEM((2, 4, 8, 128), F32),
+            pltpu.VMEM((2, 4, 8, 128), F32),
             pltpu.VMEM((ROWS * PLANES, 3, 2, 128), F32),
             pltpu.SemaphoreType.DMA,
             pltpu.SemaphoreType.DMA((3,)),
@@ -380,9 +410,8 @@
 
 
 def shards(sample_xy, sample_dz, sample_values, block_tile, block_count):
-    everything = exchange(
-        block_tile, block_count, sample_xy.reshape(8, 2, 256), sample_dz.reshape(8, 256), sample_values.reshape(8, 2, 256)
-    )
+    operands = [block_tile, block_count, sample_xy.reshape(8, 2, 256), sample_dz.reshape(8, 256), sample_values.reshape(8, 2, 256)]
+    everything = exchange(*[pltpu.with_memory_space_constraint(operand, pltpu.HBM) for operand in operands])
     block = grid_block(everything.reshape(SOURCES * SEND_ROWS, 128))
     return block.reshape(ROWS, PLANES, 2, NY)
 

time: 38.7 us -> 29.3 us (0.76)
  Pallas kernels: 34.9 us -> 29.1 us
  local copies, waits for them, and re-layouts: 3.44 us -> 0 us
    pallas_call x1, Pallas kernels: 12.2 us -> 7.01 us  [grid_block(): pl.pallas_call(kernel, out_shape=jax.ShapeDtypeStruct((ROWS * PLANES, 2,...]
    unnamed x10 -> x0, local copies, waits for them, and re-layouts: 3.44 us -> none
    pallas_call x1, Pallas kernels: 22.7 us -> 22.1 us  [exchange(): pl.pallas_call(exchange_kernel, out_shape=jax.ShapeDtypeStruct((3, GROUPS...]
where the time goes in v3:
time: 29.3 us; the launch traced here: 29.1 us
  Pallas kernels  29.1 us (99%)
    pallas_call x1, Pallas kernels, exchange(): pl.pallas_call(exchange_kernel, out_shape=jax.ShapeDtypeStruct((3, GROUPS...  22.1 us
    pallas_call x1, Pallas kernels, grid_block(): pl.pallas_call(kernel, out_shape=jax.ShapeDtypeStruct((ROWS * PLANES, 2,...  7.01 us

profile of v3, /device:TPU:1, one launch (start us, length us, event | category | flops | bytes accessed | tf_op | source)
XLA Modules:
  0.0 29.1 jit_solution(16134245811251779875)
XLA Ops:
  0.0 22.1 %exchange.1 = f32[3,8,88,128]{3,2,1,0:T(8,128)S(1)} custom-call(s32[1,1,8]{2,1,0:T(1,128)} %tile_in.1, s32[1,1,8]{2,1,0:T(1,128)} %count_in.1, f32[8,2,256]{2,1,0:T(2,128)} %bitcast.6, f32[8,256]{1,0:T(8,128)} %bitcast.8, f32[8,2,256]{2,1,0:T(2,128)} %bitcast.7), custom_call_target="tpu_custom_call" | custom-call | tf_op jit(solution)/shard_map/exchange/pallas_call | solution.py:215
  22.1 7.0 %grid_block.1 = f32[288,2,384]{2,1,0:T(2,128)} custom-call(f32[2112,128]{1,0:T(8,128)S(1)} %bitcast.5), custom_call_target="tpu_custom_call" | custom-call | tf_op jit(solution)/shard_map/grid_block/pallas_call | solution.py:392

commit v4 on v3

--- a/solution.py
+++ b/solution.py
@@ -141,9 +141,11 @@
     spot = grp - half
     peers = [half + lax.rem(spot + step, 4) for step in (2, 1, 3)]
     far_half = 4 - half
-    up = lax.rem(slab + 1, 32)
-    down = lax.rem(slab + 31, 32)
-    around = [(far, slab)] + [(peer, slab) for peer in peers] + [(grp, up), (grp, down)]
+    core = lax.rem(slab, 2)
+    outer = lax.rem(slab + 31 - 30 * core, 32)
+    inner = lax.rem(slab + 1 + 30 * core, 32)
+    beside = [((grp, outer), 2 - core), ((grp, inner), 1 + core)]
+    around = [(far, slab)] + [(peer, slab) for peer in peers] + [(grp, outer), (grp, inner)]
 
     barrier = pltpu.get_barrier_semaphore()
     for device in around:
@@ -155,56 +157,64 @@
 
     sends = []
 
-    def send(source, kind, owner, sem, device):
+    def rows_of(ref, rows):
+        return ref if rows is None else ref.at[pl.ds(rows[0], rows[1])]
+
+    def send(source, kind, owner, item, device, rows=None):
         copy = pltpu.make_async_remote_copy(
-            src_ref=source,
-            dst_ref=out_ref.at[kind, owner],
+            src_ref=rows_of(source, rows),
+            dst_ref=rows_of(out_ref.at[kind, owner], rows),
             send_sem=send_sem.at[len(sends)],
-            recv_sem=recv_sem.at[sem],
+            recv_sem=recv_sem.at[kind, item],
             device_id=device,
             device_id_type=MESH,
         )
         copy.start()
         sends.append(copy)
-        return copy
-
-    def arrive(kind, owner, sem):
+
+    def arrive(kind, owner, item, rows=None):
         pltpu.make_async_remote_copy(
-            src_ref=own_ref,
-            dst_ref=out_ref.at[kind, owner],
+            src_ref=rows_of(own_ref, rows),
+            dst_ref=rows_of(out_ref.at[kind, owner], rows),
             send_sem=send_sem.at[0],
-            recv_sem=recv_sem.at[sem],
+            recv_sem=recv_sem.at[kind, item],
             device_id=(grp, slab),
             device_id_type=MESH,
         ).wait_recv()
 
-    send(own_ref, 0, grp, 0, (far, slab))
+    pieces = [(0, HALF_ROWS), (HALF_ROWS, SEND_ROWS - HALF_ROWS)]
+    for at, rows in enumerate(pieces):
+        send(own_ref, 0, grp, 4 + at, (far, slab), rows)
     for at, peer in enumerate(peers):
         send(own_ref, 0, grp, 1 + at, (peer, slab))
-    send(own_ref, 1, grp, 7, (grp, up))
-    send(own_ref, 2, grp, 15, (grp, down))
+    for device, kind in beside:
+        send(own_ref, kind, grp, 0, device)
     out_ref[0, grp] = own_ref[...]
     back = [half + lax.rem(spot + step, 4) for step in (2, 3, 1)]
     for at in range(3):
         arrive(0, back[at], 1 + at)
-        send(out_ref.at[0, back[at]], 1, back[at], 8 + at, (grp, up))
-        send(out_ref.at[0, back[at]], 2, back[at], 16 + at, (grp, down))
-    arrive(0, far, 0)
-    for at, peer in enumerate(peers):
-        send(out_ref.at[0, far], 0, far, 4 + at, (peer, slab))
-    send(out_ref.at[0, far], 1, far, 11, (grp, up))
-    send(out_ref.at[0, far], 2, far, 19, (grp, down))
-    for at in range(3):
-        owner = back[at] - half + far_half
-        arrive(0, owner, 4 + at)
-        send(out_ref.at[0, owner], 1, owner, 12 + at, (grp, up))
-        send(out_ref.at[0, owner], 2, owner, 20 + at, (grp, down))
-    for kind, base in ((1, 7), (2, 15)):
-        arrive(kind, grp, base)
-        arrive(kind, far, base + 4)
+        for device, kind in beside:
+            send(out_ref.at[0, back[at]], kind, back[at], 1 + at, device)
+    for piece, rows in enumerate(pieces):
+        arrive(0, far, 4 + piece, rows)
+        for at, peer in enumerate(peers):
+            send(out_ref.at[0, far], 0, far, 6 + 2 * at + piece, (peer, slab), rows)
+        for device, kind in beside:
+            send(out_ref.at[0, far], kind, far, 4 + piece, device, rows)
+    for piece, rows in enumerate(pieces):
         for at in range(3):
-            arrive(kind, back[at], base + 1 + at)
-            arrive(kind, back[at] - half + far_half, base + 5 + at)
+            owner = back[at] - half + far_half
+            arrive(0, owner, 6 + 2 * at + piece, rows)
+            for device, kind in beside:
+                send(out_ref.at[0, owner], kind, owner, 6 + 2 * at + piece, device, rows)
+    for kind in (1, 2):
+        arrive(kind, grp, 0)
+        for at in range(3):
+            arrive(kind, back[at], 1 + at)
+        for piece, rows in enumerate(pieces):
+            arrive(kind, far, 4 + piece, rows)
+            for at in range(3):
+                arrive(kind, back[at] - half + far_half, 6 + 2 * at + piece, rows)
     for copy in sends:
         copy.wait_send()
 
@@ -226,8 +236,8 @@
             pltpu.VMEM((HALF_ROWS, 256), F32),
             pltpu.VMEM((SEND_ROWS, 128), F32),
             pltpu.SemaphoreType.DMA((5,)),
-            pltpu.SemaphoreType.DMA((23,)),
-            pltpu.SemaphoreType.DMA((23,)),
+            pltpu.SemaphoreType.DMA((35,)),
+            pltpu.SemaphoreType.DMA((3, 12)),
         ],
         compiler_params=pltpu.CompilerParams(collective_id=0, has_side_effects=True, vmem_limit_bytes=8 * 2**20),
         name="exchange",
@@ -283,11 +293,15 @@
         return body
 
     offset = jnp.int32(0)
-    for wrap in (False, True):
-        for kind in range(3):
-            steps = jnp.where(group == GROUPS - 1, GROUPS, 0) if wrap else GROUPS
-            offset, more = lax.fori_loop(0, steps, gather(kind, wrap), (offset, jnp.int32(0)))
-            offset = lax.fori_loop(0, jnp.where(more > 0, 64, 0), gather_rest(kind, wrap), offset)
+    for kind in range(3):
+        more = jnp.int32(0)
+        for at in range(GROUPS):
+            offset, more = gather(kind, False)(at, (offset, more))
+        offset = lax.fori_loop(0, jnp.where(more > 0, 64, 0), gather_rest(kind, False), offset)
+    for kind in range(3):
+        steps = jnp.where(group == GROUPS - 1, GROUPS, 0)
+        offset, more = lax.fori_loop(0, steps, gather(kind, True), (offset, jnp.int32(0)))
+        offset = lax.fori_loop(0, jnp.where(more > 0, 64, 0), gather_rest(kind, True), offset)
 
     subs_f = subs.astype(F32)
     first_row = (group * ROWS).astype(F32)

time: 29.3 us -> 28.5 us (0.973)
  Pallas kernels: 29.1 us -> 28.5 us
    pallas_call x1, Pallas kernels: 7.01 us -> 6.45 us  [grid_block(): pl.pallas_call(kernel, out_shape=jax.ShapeDtypeStruct((ROWS * PLANES, 2,...]
where the time goes in v4:
time: 28.5 us
  Pallas kernels  28.5 us (100%)
    pallas_call x1, Pallas kernels, exchange(): pl.pallas_call(exchange_kernel, out_shape=jax.ShapeDtypeStruct((3, GROUPS...  22.1 us
    pallas_call x1, Pallas kernels, grid_block(): pl.pallas_call(kernel, out_shape=jax.ShapeDtypeStruct((ROWS * PLANES, 2,...  6.45 us

profile of v4, /device:TPU:1, one launch (start us, length us, event | category | flops | bytes accessed | tf_op | source)
XLA Modules:
  0.0 28.5 jit_solution(2712862345232638767)
XLA Ops:
  0.0 22.1 %exchange.1 = f32[3,8,88,128]{3,2,1,0:T(8,128)S(1)} custom-call(s32[1,1,8]{2,1,0:T(1,128)} %tile_in.1, s32[1,1,8]{2,1,0:T(1,128)} %count_in.1, f32[8,2,256]{2,1,0:T(2,128)} %bitcast.6, f32[8,256]{1,0:T(8,128)} %bitcast.8, f32[8,2,256]{2,1,0:T(2,128)} %bitcast.7), custom_call_target="tpu_custom_call" | custom-call | tf_op jit(solution)/shard_map/exchange/pallas_call | solution.py:225
  22.1 6.5 %grid_block.1 = f32[288,2,384]{2,1,0:T(2,128)} custom-call(f32[2112,128]{1,0:T(8,128)S(1)} %bitcast.5), custom_call_target="tpu_custom_call" | custom-call | tf_op jit(solution)/shard_map/grid_block/pallas_call | solution.py:406

commit v5 on v4

--- a/solution.py
+++ b/solution.py
@@ -18,7 +18,9 @@
 TABLE = 2 * HALF_ROWS
 SEND_ROWS = TABLE + BLOCKS
 SOURCES = 3 * GROUPS
-START, COUNT, LEFT, WRAP, WRAP_LEFT, ANY_LEFT = 0, 8, 32, 56, 80, 104
+LOW, COUNT, LEFT, WRAP, WRAP_LEFT, ANY_LEFT, HIGH = 0, 8, 32, 56, 80, 104, 112
+PIECES = [(0, HALF_ROWS), (HALF_ROWS, SEND_ROWS - HALF_ROWS)]
+ORDER = (1, 2, 0)
 MESH = pl.DeviceIdType.MESH
 BETA = math.pi * math.sqrt(19.45)
 F32 = jnp.float32
@@ -87,7 +89,10 @@
         start = below(float(ROWS * group))
         count = below(float(ROWS * group + ROWS + 5)) - start
         first = jnp.minimum(count, 128.0)
-        table = jnp.where(column == START + group, jnp.minimum(start, 255.0), table)
+        start = jnp.minimum(start, 255.0)
+        high = jnp.where(start > 127.5, 1.0, 0.0)
+        table = jnp.where(column == LOW + group, start - 128.0 * high, table)
+        table = jnp.where(column == HIGH + group, high * HALF_ROWS, table)
         for kind in range(3):
             table = jnp.where(column == COUNT + 8 * kind + group, first * kinds[kind], table)
             table = jnp.where(column == LEFT + 8 * kind + group, (count - first) * kinds[kind], table)
@@ -101,6 +106,7 @@
     pieces += [jnp.broadcast_to(table[WRAP + at : WRAP + at + 1], (8, 8)) for at in range(6)]
     left = pieces[4] + pieces[10]
     pieces.append(jnp.broadcast_to(jnp.sum(left, axis=1, keepdims=True), (8, 8)))
+    pieces.append(table[HIGH : HIGH + 8])
     out_ref[TABLE : TABLE + BLOCKS, :] = jnp.concatenate(pieces + [jnp.zeros((8, 128 - 8 * len(pieces)), F32)], axis=1)
     key = shifted * 256.0 + lanes.astype(F32)
     key_t = key.T
@@ -182,7 +188,8 @@
             device_id_type=MESH,
         ).wait_recv()
 
-    pieces = [(0, HALF_ROWS), (HALF_ROWS, SEND_ROWS - HALF_ROWS)]
+    pieces = PIECES
+    count = len(pieces)
     for at, rows in enumerate(pieces):
         send(own_ref, 0, grp, 4 + at, (far, slab), rows)
     for at, peer in enumerate(peers):
@@ -191,22 +198,22 @@
         send(own_ref, kind, grp, 0, device)
     out_ref[0, grp] = own_ref[...]
     back = [half + lax.rem(spot + step, 4) for step in (2, 3, 1)]
-    for at in range(3):
+    for at in ORDER:
         arrive(0, back[at], 1 + at)
         for device, kind in beside:
             send(out_ref.at[0, back[at]], kind, back[at], 1 + at, device)
     for piece, rows in enumerate(pieces):
         arrive(0, far, 4 + piece, rows)
         for at, peer in enumerate(peers):
-            send(out_ref.at[0, far], 0, far, 6 + 2 * at + piece, (peer, slab), rows)
+            send(out_ref.at[0, far], 0, far, 4 + count + count * at + piece, (peer, slab), rows)
         for device, kind in beside:
             send(out_ref.at[0, far], kind, far, 4 + piece, device, rows)
     for piece, rows in enumerate(pieces):
-        for at in range(3):
+        for at in ORDER:
             owner = back[at] - half + far_half
-            arrive(0, owner, 6 + 2 * at + piece, rows)
+            arrive(0, owner, 4 + count + count * at + piece, rows)
             for device, kind in beside:
-                send(out_ref.at[0, owner], kind, owner, 6 + 2 * at + piece, device, rows)
+                send(out_ref.at[0, owner], kind, owner, 4 + count + count * at + piece, device, rows)
     for kind in (1, 2):
         arrive(kind, grp, 0)
         for at in range(3):
@@ -214,7 +221,7 @@
         for piece, rows in enumerate(pieces):
             arrive(kind, far, 4 + piece, rows)
             for at in range(3):
-                arrive(kind, back[at] - half + far_half, 6 + 2 * at + piece, rows)
+                arrive(kind, back[at] - half + far_half, 4 + count + count * at + piece, rows)
     for copy in sends:
         copy.wait_send()
 
@@ -236,8 +243,8 @@
             pltpu.VMEM((HALF_ROWS, 256), F32),
             pltpu.VMEM((SEND_ROWS, 128), F32),
             pltpu.SemaphoreType.DMA((5,)),
-            pltpu.SemaphoreType.DMA((35,)),
-            pltpu.SemaphoreType.DMA((3, 12)),
+            pltpu.SemaphoreType.DMA((11 + 12 * len(PIECES),)),
+            pltpu.SemaphoreType.DMA((3, 4 + 4 * len(PIECES))),
         ],
         compiler_params=pltpu.CompilerParams(collective_id=0, has_side_effects=True, vmem_limit_bytes=8 * 2**20),
         name="exchange",
@@ -255,11 +262,9 @@
     subs = lax.broadcasted_iota(I32, (8, 128), 0)
     copy.wait()
 
-    def append(kind, source, b, start, count, offset):
+    def append(kind, source, b, low, rows, count, offset):
         first = source * SEND_ROWS + b
-        low = lax.bitwise_and(start, 127)
-        half = lax.shift_right_logical(start, 7)
-        values = all_ref[pl.ds(first + half * HALF_ROWS, FIELDS, stride=8), :]
+        values = all_ref[pl.ds(first + rows, FIELDS, stride=8), :]
         after = all_ref[pl.ds(first + HALF_ROWS, FIELDS, stride=8), :]
         values = jnp.where(lanes_f >= low, values, after)
         if kind > 0:
@@ -271,13 +276,16 @@
         packed[slot + 1, 0:FIELDS] = rolled
         return offset + count
 
+    def span(wrap, source, b):
+        return (jnp.int32(0), jnp.int32(0)) if wrap else (table[source, LOW + b], table[source, HIGH + b])
+
     def gather(kind, wrap):
         def body(at, carry):
             offset, more = carry
             source = kind * GROUPS + at
             for b in range(BLOCKS):
-                start = jnp.int32(0) if wrap else table[source, START + b]
-                offset = append(kind, source, b, start, table[source, (WRAP if wrap else COUNT) + 8 * kind + b], offset)
+                low, rows = span(wrap, source, b)
+                offset = append(kind, source, b, low, rows, table[source, (WRAP if wrap else COUNT) + 8 * kind + b], offset)
             return offset, more + table[source, ANY_LEFT]
 
         return body
@@ -286,9 +294,9 @@
         def body(at, offset):
             source = kind * GROUPS + lax.shift_right_logical(at, 3)
             b = lax.bitwise_and(at, 7)
-            start = jnp.int32(0) if wrap else table[source, START + b]
+            low = span(wrap, source, b)[0]
             left = table[source, (WRAP_LEFT if wrap else LEFT) + 8 * kind + b]
-            return lax.cond(left > 0, lambda o: append(kind, source, b, start + 128, left, o), lambda o: o, offset)
+            return lax.cond(left > 0, lambda o: append(kind, source, b, low, HALF_ROWS, left, o), lambda o: o, offset)
 
         return body
 
@@ -372,9 +380,18 @@
             prepare(held0, at * 2 + 2)
             return carry
 
-        lax.fori_loop(0, lax.shift_right_logical(offset + 511, 9), two_chunks, 0)
-        for unit in range(2):
-            pltpu.matmul_acc_lhs(sums[unit][0], jnp.zeros((ROWS, 256), BF16), load_staged_rhs=0)
+        chunks = lax.shift_right_logical(offset + 255, 8)
+        lax.fori_loop(0, lax.shift_right_logical(chunks, 1), two_chunks, 0)
+
+        @pl.when(lax.bitwise_and(chunks, 1) == 1)
+        def _():
+            stream(held0, sums)
+
+        @pl.when(lax.bitwise_and(chunks, 1) == 0)
+        def _():
+            for unit in range(2):
+                pltpu.matmul_acc_lhs(sums[unit][0], jnp.zeros((ROWS, 256), BF16), load_staged_rhs=0)
+
         lines = flat.reshape(ROWS * PLANES * 6, 128)
         for plane in range(2 * PLANES):
             z, c = plane // 2, plane % 2

time: 28.5 us -> 27.7 us (0.972)
  Pallas kernels: 28.5 us -> 27.7 us
    pallas_call x1, Pallas kernels: 22.1 us -> 21.6 us  [exchange(): pl.pallas_call(exchange_kernel, out_shape=jax.ShapeDtypeStruct((3, GROUPS...]
    pallas_call x1, Pallas kernels: 6.45 us -> 6.07 us  [grid_block(): pl.pallas_call(kernel, out_shape=jax.ShapeDtypeStruct((ROWS * PLANES, 2,...]
where the time goes in v5:
time: 27.7 us
  Pallas kernels  27.7 us (100%)
    pallas_call x1, Pallas kernels, exchange(): pl.pallas_call(exchange_kernel, out_shape=jax.ShapeDtypeStruct((3, GROUPS...  21.6 us
    pallas_call x1, Pallas kernels, grid_block(): pl.pallas_call(kernel, out_shape=jax.ShapeDtypeStruct((ROWS * PLANES, 2,...  6.07 us

profile of v5, /device:TPU:1, one launch (start us, length us, event | category | flops | bytes accessed | tf_op | source)
XLA Modules:
  0.0 27.7 jit_solution(15467622262578328305)
XLA Ops:
  0.0 21.6 %exchange.1 = f32[3,8,88,128]{3,2,1,0:T(8,128)S(1)} custom-call(s32[1,1,8]{2,1,0:T(1,128)} %tile_in.1, s32[1,1,8]{2,1,0:T(1,128)} %count_in.1, f32[8,2,256]{2,1,0:T(2,128)} %bitcast.6, f32[8,256]{1,0:T(8,128)} %bitcast.8, f32[8,2,256]{2,1,0:T(2,128)} %bitcast.7), custom_call_target="tpu_custom_call" | custom-call | tf_op jit(solution)/shard_map/exchange/pallas_call | solution.py:232
  21.6 6.1 %grid_block.1 = f32[288,2,384]{2,1,0:T(2,128)} custom-call(f32[2112,128]{1,0:T(8,128)S(1)} %bitcast.5), custom_call_target="tpu_custom_call" | custom-call | tf_op jit(solution)/shard_map/grid_block/pallas_call | solution.py:423

commit v6 on v5

--- a/solution.py
+++ b/solution.py
@@ -300,16 +300,20 @@
 
         return body
 
-    offset = jnp.int32(0)
-    for kind in range(3):
+    def gather_kind(kind, offset):
         more = jnp.int32(0)
         for at in range(GROUPS):
             offset, more = gather(kind, False)(at, (offset, more))
-        offset = lax.fori_loop(0, jnp.where(more > 0, 64, 0), gather_rest(kind, False), offset)
-    for kind in range(3):
-        steps = jnp.where(group == GROUPS - 1, GROUPS, 0)
-        offset, more = lax.fori_loop(0, steps, gather(kind, True), (offset, jnp.int32(0)))
-        offset = lax.fori_loop(0, jnp.where(more > 0, 64, 0), gather_rest(kind, True), offset)
+        return offset, more
+
+    def gather_others(offset, left):
+        for kind in range(3):
+            offset = lax.fori_loop(0, jnp.where(left[kind] > 0, 64, 0), gather_rest(kind, False), offset)
+        for kind in range(3):
+            steps = jnp.where(group == GROUPS - 1, GROUPS, 0)
+            offset, more = lax.fori_loop(0, steps, gather(kind, True), (offset, jnp.int32(0)))
+            offset = lax.fori_loop(0, jnp.where(more > 0, 64, 0), gather_rest(kind, True), offset)
+        return offset
 
     subs_f = subs.astype(F32)
     first_row = (group * ROWS).astype(F32)
@@ -331,7 +335,7 @@
 
     zero = jnp.zeros((16, 128), BF16)
 
-    def prepare(held, at):
+    def prepare(held, at, offset):
         sides = []
         for half in range(2):
             values = packed[at * 2 + half]
@@ -371,17 +375,37 @@
 
     def run(*accumulators):
         sums = (accumulators[:12], accumulators[12:])
-        prepare(held0, 0)
+        own, left_own = gather_kind(0, jnp.int32(0))
+
+        def gather_beside(offset):
+            offset, left_below = gather_kind(1, offset)
+            offset, left_above = gather_kind(2, offset)
+            return offset, left_below, left_above
+
+        def with_chunks(offset):
+            prepare(held0, 0, offset)
+            prepare_next = offset
+            stream(held0, sums)
+            offset, left_below = gather_kind(1, offset)
+            prepare(held1, 1, prepare_next)
+            stream(held1, sums)
+            offset, left_above = gather_kind(2, offset)
+            return offset, left_below, left_above
+
+        offset, left_below, left_above = lax.cond(own >= 512, with_chunks, gather_beside, own)
+        offset = gather_others(offset, (left_own, left_below, left_above))
+        done = jnp.where(own >= 512, 1, 0)
+        prepare(held0, done * 2, offset)
 
         def two_chunks(at, carry):
             stream(held0, sums)
-            prepare(held1, at * 2 + 1)
+            prepare(held1, at * 2 + 1, offset)
             stream(held1, sums)
-            prepare(held0, at * 2 + 2)
+            prepare(held0, at * 2 + 2, offset)
             return carry
 
         chunks = lax.shift_right_logical(offset + 255, 8)
-        lax.fori_loop(0, lax.shift_right_logical(chunks, 1), two_chunks, 0)
+        lax.fori_loop(done, lax.shift_right_logical(chunks, 1), two_chunks, 0)
 
         @pl.when(lax.bitwise_and(chunks, 1) == 1)
         def _():

time: 27.7 us -> 27.3 us (0.986)
  Pallas kernels: 27.7 us -> 27.3 us
    pallas_call x1, Pallas kernels: 6.07 us -> 5.65 us  [grid_block(): pl.pallas_call(kernel, out_shape=jax.ShapeDtypeStruct((ROWS * PLANES, 2,...]
where the time goes in v6:
time: 27.3 us
  Pallas kernels  27.3 us (100%)
    pallas_call x1, Pallas kernels, exchange(): pl.pallas_call(exchange_kernel, out_shape=jax.ShapeDtypeStruct((3, GROUPS...  21.6 us
    pallas_call x1, Pallas kernels, grid_block(): pl.pallas_call(kernel, out_shape=jax.ShapeDtypeStruct((ROWS * PLANES, 2,...  5.65 us

profile of v6, /device:TPU:1, one launch (start us, length us, event | category | flops | bytes accessed | tf_op | source)
XLA Modules:
  0.0 27.3 jit_solution(15707287728086939432)
XLA Ops:
  0.0 21.6 %exchange.1 = f32[3,8,88,128]{3,2,1,0:T(8,128)S(1)} custom-call(s32[1,1,8]{2,1,0:T(1,128)} %tile_in.1, s32[1,1,8]{2,1,0:T(1,128)} %count_in.1, f32[8,2,256]{2,1,0:T(2,128)} %bitcast.6, f32[8,256]{1,0:T(8,128)} %bitcast.8, f32[8,2,256]{2,1,0:T(2,128)} %bitcast.7), custom_call_target="tpu_custom_call" | custom-call | tf_op jit(solution)/shard_map/exchange/pallas_call | solution.py:232
  21.6 5.7 %grid_block.1 = f32[288,2,384]{2,1,0:T(2,128)} custom-call(f32[2112,128]{1,0:T(8,128)S(1)} %bitcast.5), custom_call_target="tpu_custom_call" | custom-call | tf_op jit(solution)/shard_map/grid_block/pallas_call | solution.py:447
